TPU v7x, 8 devices: a whole 2x2x1 slice. The times are simulated.
8 devices in a mesh: batch: 2 (over z, y), dap: 4 (over x, core).
Axes of the slice: x: 2, y: 2, z: 1, core: 2. Of those that a mesh axis runs over, the one named last changes fastest.
Arguments:
- z_pair: bfloat16 [1024, 512, 128], P(('batch', 'dap')), parts along dimension 0
- pair_mask: int32 [1024, 512], P(('batch', 'dap')), parts along dimension 0
- dz_out: bfloat16 [1024, 512, 128], P(('batch', 'dap')), parts along dimension 0
- ln_in_scale: bfloat16 [128], replicated
- ln_in_offset: bfloat16 [128], replicated
- w_in: bfloat16 [128, 512], replicated
- b_in: bfloat16 [512], replicated
- ln_out_scale: bfloat16 [128], replicated
- ln_out_offset: bfloat16 [128], replicated
- w_out: bfloat16 [128, 128], replicated
- b_out: bfloat16 [128], replicated
- w_gate: bfloat16 [128, 128], replicated
- b_gate: bfloat16 [128], replicated
Outputs:
- output 1: bfloat16 [1024, 512, 128], P(('batch', 'dap')), parts along dimension 0
- output 2: bfloat16 [256], P('batch'), parts along dimension 0
- output 3: bfloat16 [256], P('batch'), parts along dimension 0
- output 4: bfloat16 [256, 512], P('batch'), parts along dimension 0
- output 5: bfloat16 [1024], P('batch'), parts along dimension 0
- output 6: bfloat16 [256], P('batch'), parts along dimension 0
- output 7: bfloat16 [256], P('batch'), parts along dimension 0
- output 8: bfloat16 [256, 128], P('batch'), parts along dimension 0
- output 9: bfloat16 [256], P('batch'), parts along dimension 0
- output 10: bfloat16 [256, 128], P('batch'), parts along dimension 0
- output 11: bfloat16 [256], P('batch'), parts along dimension 0
There are 2 independent parts. A program takes and returns all parts, laid end to end along the dimension named above; an argument that names none is the same for every part.
All inputs are finite; a program needn't handle non-finite values.
Results may differ from a plain program's by a relative error of at most 0.0133434.
Values are sent between devices in bfloat16 or wider.
A program may use at most 1 GiB of HBM per device.

v0:
```python
import functools
import jax
import jax.numpy as jnp
from jax import lax
from jax.experimental import pallas as pl
from jax.experimental.pallas import tpu as pltpu
from jax.sharding import PartitionSpec as P

LN_EPS = 1e-5
F32 = jnp.float32
BF16 = jnp.bfloat16
LANES = 128
ROWS = 16
MID_CH = 16
MID_ROWS = 32
GROUP = 16
VMEM_LIMIT = 60 * 1024 * 1024


def col_mean(x_val):
    return jnp.sum(x_val, axis=0, keepdims=True) * (1.0 / x_val.shape[0])


def dot_nn(lhs, rhs):
    return jnp.dot(lhs, rhs, preferred_element_type=F32)


def dot_nt(lhs, rhs):
    return lax.dot_general(lhs, rhs, (((1,), (1,)), ((), ())), preferred_element_type=F32)


def dot_tn(lhs, rhs):
    return lax.dot_general(lhs, rhs, (((0,), (0,)), ((), ())), preferred_element_type=F32)


def input_norm(z_rows, scale, offset):
    z_t = jnp.transpose(z_rows.astype(F32))
    centered = z_t - col_mean(z_t)
    inv_std = lax.rsqrt(col_mean(centered * centered) + LN_EPS)
    x_hat = centered * inv_std
    return x_hat, inv_std, (x_hat * scale + offset).astype(BF16)


def with_bias(mat, vec):
    pad = jnp.zeros((mat.shape[0], LANES - 1), BF16)
    return jnp.concatenate([mat, vec[:, None], pad], axis=1)


def by_group(arr):
    split = arr.reshape(arr.shape[:-1] + (4, -1, GROUP))
    return jnp.swapaxes(split, -3, -2).reshape(arr.shape)


def from_group(arr):
    split = arr.reshape(arr.shape[:-1] + (-1, 4, GROUP))
    return jnp.swapaxes(split, -3, -2).reshape(arr.shape)


def ones_row(width):
    return (lax.broadcasted_iota(jnp.int32, (LANES, width), 0) == 0).astype(F32).astype(BF16)


def project_kernel(keep_norm, z_ref, mask_ref, w_ref, scale_ref, offset_ref, *refs):
    refs = refs[-5:] if keep_norm else refs[-4:]
    a_ref, b_ref = refs[:2]
    scr_a, scr_b = refs[-2:]
    n_lane = z_ref.shape[1] // LANES
    chans = z_ref.shape[2]
    pitch = ROWS + 1
    plane = chans * pitch
    one16 = ones_row(256)

    def row(i, carry):
        for half in range(n_lane // 2):
            cols = slice(half * 256, half * 256 + 256)
            _, _, znt = input_norm(z_ref[i, cols, :], scale_ref[...], offset_ref[...])
            if keep_norm:
                refs[2][i, cols, :] = jnp.transpose(znt)
            mask16 = jnp.concatenate([mask_ref[i, half * 2 + t] for t in range(2)], axis=1).astype(F32).astype(BF16)
            proj = dot_nn(w_ref[...], jnp.concatenate([znt * mask16, one16 * mask16], axis=0))
            for g in range(chans // GROUP):
                pa, pb, la, lb = [proj[(4 * g + n) * GROUP:(4 * g + n + 1) * GROUP] for n in range(4)]
                for scr, val in ((scr_a, jax.nn.sigmoid(la) * pa), (scr_b, jax.nn.sigmoid(lb) * pb)):
                    for t in range(2):
                        at = (half * 2 + t) * plane + g * GROUP * pitch + i
                        scr[pl.ds(at, GROUP, stride=pitch), :] = val[:, t * LANES:(t + 1) * LANES]
        return carry

    lax.fori_loop(0, ROWS, row, 0)

    def pack(c, carry):
        for t in range(n_lane):
            lanes = slice(t * LANES, (t + 1) * LANES)
            at = t * plane + c * pitch
            a_ref[c, :, lanes] = scr_a[pl.ds(at, ROWS), :].astype(BF16)
            b_ref[c, :, lanes] = scr_b[pl.ds(at, ROWS), :].astype(BF16)
        return carry

    lax.fori_loop(0, chans, pack, 0, unroll=4)


def project(z_rows, mask_rows, first, rows, w_t, scale, offset, keep_norm, after=()):
    _, n_col, chans = z_rows.shape
    z_from, m_from = (0 if z_rows.shape[0] == rows else first // ROWS), first // ROWS
    full = lambda arr: pl.BlockSpec(arr.shape, lambda s: (0,) * arr.ndim)
    act = jax.ShapeDtypeStruct((chans, rows, n_col), BF16)
    act_spec = pl.BlockSpec((chans, ROWS, n_col), lambda s: (0, s, 0))
    out_shape = [act, act]
    out_specs = [act_spec, act_spec]
    pair_spec = pl.BlockSpec((ROWS, n_col, chans), lambda s: (s + z_from, 0, 0))
    if keep_norm:
        out_shape.append(jax.ShapeDtypeStruct((rows, n_col, chans), BF16))
        out_specs.append(pair_spec)
    scratch = pltpu.VMEM((n_col // LANES * chans * (ROWS + 1), LANES), F32)
    return pl.pallas_call(
        functools.partial(project_kernel, keep_norm),
        grid=(rows // ROWS,),
        in_specs=[
            pair_spec,
            pl.BlockSpec((ROWS,) + mask_rows.shape[1:], lambda s: (s + m_from, 0, 0, 0)),
            full(w_t), full(scale), full(offset)] + [pl.BlockSpec(memory_space=pl.ANY)] * len(after),
        out_specs=out_specs,
        out_shape=out_shape,
        scratch_shapes=[scratch, scratch],
        compiler_params=pltpu.CompilerParams(vmem_limit_bytes=VMEM_LIMIT),
        cost_estimate=pl.CostEstimate(flops=rows * 2 * 10 ** 8, bytes_accessed=rows * 2 ** 19, transcendentals=0),
        name='project',
    )(z_rows, mask_rows, w_t, scale, offset, *after)


def middle_kernel(n_mul, n_mid, n_part, idx_ref, a_ref, *refs):
    b_refs = refs[:n_part]
    zn0_ref, zn1_ref, dy0_ref, dy1_ref, wg_ref, wo_ref, wot_ref, scale_ref, offset_ref = refs[n_part:n_part + 9]
    do0_ref, do1_ref, gl_ref, dwo_ref, dwg_ref, vec_ref, scr = refs[-7:]
    step = pl.program_id(0)
    tile = LANES
    half = tile // 2
    pitch = tile + 1
    chans = wo_ref.shape[0]

    one16 = ones_row(2 * tile)
    one_col = (lax.broadcasted_iota(jnp.int32, (2 * tile, LANES), 1) == 0).astype(F32).astype(BF16)

    @pl.when(step == 0)
    def _():
        dwo_ref[...] = jnp.zeros_like(dwo_ref)
        dwg_ref[...] = jnp.zeros_like(dwg_ref)
        vec_ref[...] = jnp.zeros_like(vec_ref)

    @pl.when(step < n_mul)
    def _():
        for j in range(MID_CH):
            at = (step * MID_CH + j) * pitch
            scr[pl.ds(at, tile), :] = dot_nt(a_ref[j], jnp.concatenate([ref[j] for ref in b_refs], axis=0))

    @pl.when((step >= n_mul) & (step < n_mul + n_mid))
    def _():
        first = (step - n_mul) * MID_ROWS

        def pair(h, carry):
            r0 = first + 2 * h
            tri = jnp.concatenate([scr[pl.ds(r0 + t, chans, stride=pitch), :] for t in range(2)], axis=1)
            centered = tri - col_mean(tri)
            inv_std = lax.rsqrt(col_mean(centered * centered) + LN_EPS)
            o_hat = centered * inv_std
            o_norm = (o_hat * scale_ref[...] + offset_ref[...]).astype(BF16)
            update = dot_nn(wot_ref[...], jnp.concatenate([o_norm, one16], axis=0)).astype(BF16).astype(F32)
            zn = jnp.concatenate([ref[2 * h + t] for t in range(2) for ref in (zn0_ref, zn1_ref)], axis=0)
            sig_g = jax.nn.sigmoid(dot_nt(wg_ref[...], jnp.concatenate([zn, one_col], axis=1)))
            dy_t = jnp.transpose(jnp.concatenate([ref[2 * h + t].astype(F32) for t in range(2) for ref in (dy0_ref, dy1_ref)], axis=0))
            d_update = (sig_g * dy_t).astype(BF16)
            d_gate = dy_t * update * sig_g * (1.0 - sig_g)
            gate16 = d_gate.astype(BF16)
            d_onorm = dot_nn(wo_ref[...], d_update).astype(BF16).astype(F32)
            grad_hat = d_onorm * scale_ref[...]
            d_tri = inv_std * (grad_hat - col_mean(grad_hat) - o_hat * col_mean(grad_hat * o_hat))
            d_upf = d_update.astype(F32)
            d_sc = d_onorm * o_hat
            for t in range(2):
                part = slice(t * tile, (t + 1) * tile)
                scr[pl.ds(r0 + t, chans, stride=pitch), :] = d_tri[:, part]
                gl_ref[2 * h + t] = gate16[:, part]
            vec_ref[0] += d_sc[:, :tile] + d_sc[:, tile:]
            vec_ref[1] += d_onorm[:, :tile] + d_onorm[:, tile:]
            vec_ref[2] += d_upf[:, :tile] + d_upf[:, tile:]
            vec_ref[3] += d_gate[:, :tile] + d_gate[:, tile:]
            dwo_ref[...] += dot_nt(o_norm, d_update)
            dwg_ref[...] += dot_nn(gate16, zn)
            return carry

        lax.fori_loop(0, MID_ROWS // 2, pair, 0)

    @pl.when(step >= n_mul + n_mid)
    def _():
        for j in range(MID_CH):
            at = ((step - n_mul - n_mid) * MID_CH + j) * pitch
            do_t = jnp.transpose(scr[pl.ds(at, tile), :]).astype(BF16)
            do0_ref[j] = do_t[:half]
            do1_ref[j] = do_t[half:]


def middle(pieces, act_a, b_parts, zn, dy_rows, wg_t, wo, wo_t, scale, offset, after=()):
    chans, rows, n_col = act_a.shape
    half = LANES // 2
    n_mul = chans // MID_CH
    n_mid = rows // MID_ROWS
    mul_at = lambda s: jnp.minimum(s, n_mul - 1)
    mid_at = lambda s: jnp.clip(s - n_mul, 0, n_mid - 1)
    out_at = lambda s: jnp.maximum(s - n_mul - n_mid, 0)
    full = lambda shape: pl.BlockSpec(shape, lambda s, q: (0,) * len(shape))
    part_spec = lambda arr: pl.BlockSpec((MID_CH,) + arr.shape[1:], lambda s, q: (mul_at(s), 0, 0))
    piece_spec = lambda n: pl.BlockSpec((MID_ROWS, half, chans), lambda s, q: (mid_at(s), q[n], 0))
    do_spec = pl.BlockSpec((MID_CH, half, rows), lambda s, q: (out_at(s), 0, 0))
    do_type = jax.ShapeDtypeStruct((chans, half, rows), BF16)
    mats = jax.ShapeDtypeStruct((chans, chans), F32)
    return pl.pallas_call(
        functools.partial(middle_kernel, n_mul, n_mid, len(b_parts)),
        grid_spec=pltpu.PrefetchScalarGridSpec(
            num_scalar_prefetch=1,
            grid=(2 * n_mul + n_mid,),
            in_specs=[
                pl.BlockSpec((MID_CH, rows, n_col), lambda s, q: (mul_at(s), 0, 0)),
                *[part_spec(arr) for arr in b_parts],
                piece_spec(0), piece_spec(1), piece_spec(0), piece_spec(1),
                full(wg_t.shape), full(wo.shape), full(wo_t.shape), full(scale.shape), full(offset.shape)]
            + [pl.BlockSpec(memory_space=pl.ANY)] * len(after),
            out_specs=[
                do_spec, do_spec,
                pl.BlockSpec((MID_ROWS, chans, LANES), lambda s, q: (mid_at(s), 0, 0)),
                full((chans, chans)), full((chans, chans)), full((4, chans, LANES))],
            scratch_shapes=[pltpu.VMEM((chans * (LANES + 1), LANES), F32)],
        ),
        out_shape=[
            do_type, do_type,
            jax.ShapeDtypeStruct((rows, chans, LANES), BF16),
            mats, mats, jax.ShapeDtypeStruct((4, chans, LANES), F32)],
        compiler_params=pltpu.CompilerParams(vmem_limit_bytes=VMEM_LIMIT),
        cost_estimate=pl.CostEstimate(flops=25 * 10 ** 9, bytes_accessed=48 * 2 ** 20, transcendentals=0),
        name='middle',
    )(pieces, act_a, *b_parts, zn, zn, dy_rows, dy_rows, wg_t, wo, wo_t, scale, offset, *after)


def grad_kernel(trans, n_do, n_act, n_seed, partial, *refs):
    grads, acts, rest = refs[:n_do], refs[n_do:n_do + n_act], refs[n_do + n_act:]
    step = acts[0].shape[0]
    pitch = step + 1

    def product(c):
        if trans:
            lhs = jnp.concatenate([g[c] for g in grads], axis=0)
        else:
            lhs = jnp.concatenate([jnp.concatenate([g[c] for g in grads[n:n + 2]], axis=1) for n in range(0, n_do, 2)], axis=0)
        rhs = jnp.concatenate([act[c] for act in acts], axis=0)
        acc = dot_tn(lhs, rhs) if trans else dot_nn(lhs, rhs)
        return acc + rest[0][c] if n_seed else acc

    if partial:
        out_ref = rest[-1]

        def block(n, carry):
            for j in range(4):
                out_ref[4 * n + j] = product(4 * n + j)
            return carry

        lax.fori_loop(0, step // 4, block, 0)
        return
    mask_ref, out_ref, scr = rest[n_seed], rest[-2], rest[-1]
    rows, n_col = mask_ref.shape
    plane = rows * pitch

    def block(n, carry):
        for j in range(4):
            acc = product(4 * n + j) * mask_ref[...]
            for t in range(n_col // LANES):
                scr[pl.ds(t * plane + 4 * n + j, rows, stride=pitch), :] = acc[:, t * LANES:(t + 1) * LANES]
        return carry

    lax.fori_loop(0, step // 4, block, 0)

    def pack(i, carry):
        for t in range(n_col // LANES):
            out_ref[i, :, t * LANES:(t + 1) * LANES] = scr[pl.ds(t * plane + i * pitch, step), :].astype(BF16)
        return carry

    lax.fori_loop(0, rows, pack, 0, unroll=8)


def grad_sum(trans, grads, acts, mask_f, part=0, parts=1, seed=None, partial=False, after=()):
    chans = grads[0].shape[0]
    n_col = acts[0].shape[2]
    rows = mask_f.shape[0] // parts
    step = MID_CH
    block = lambda arr: pl.BlockSpec((step,) + arr.shape[1:], lambda s: (s, 0, 0))
    sum_spec = lambda at: pl.BlockSpec((step, rows, n_col), lambda s: (s, at, 0))
    seeds = [] if seed is None else [seed]
    if partial:
        masks, scratch = [], []
        out_spec, out_shape = sum_spec(0), jax.ShapeDtypeStruct((chans, rows, n_col), F32)
    else:
        masks, scratch = [mask_f], [pltpu.VMEM((n_col // LANES * rows * (step + 1), LANES), F32)]
        out_spec = pl.BlockSpec((rows, step, n_col), lambda s: (0, s, 0))
        out_shape = jax.ShapeDtypeStruct((rows, chans, n_col), BF16)
    return pl.pallas_call(
        functools.partial(grad_kernel, trans, len(grads), len(acts), len(seeds), partial),
        grid=(chans // step,),
        in_specs=[block(arr) for arr in list(grads) + list(acts)] + [sum_spec(part)] * len(seeds)
        + [pl.BlockSpec((rows, n_col), lambda s: (part, 0))] * len(masks) + [pl.BlockSpec(memory_space=pl.ANY)] * len(after),
        out_specs=out_spec,
        out_shape=out_shape,
        scratch_shapes=scratch,
        compiler_params=pltpu.CompilerParams(vmem_limit_bytes=VMEM_LIMIT),
        cost_estimate=pl.CostEstimate(flops=12 * 10 ** 9, bytes_accessed=80 * 2 ** 20, transcendentals=0),
    )(*grads, *acts, *seeds, *masks, *after)


def final_kernel(seeded, q_ref, z_ref, dy_ref, da_ref, db_ref, gl0, gl1, gl2, gl3, w_ref, wb_ref, scale_ref, offset_ref, *refs):
    dz_ref, dw_ref, dbin_ref, vec_ref = refs[-4:]
    gls = (gl0, gl1, gl2, gl3)
    chans = z_ref.shape[2]
    n_lane = z_ref.shape[1] // LANES
    side = LANES // 2

    @pl.when(pl.program_id(0) == 0)
    def _():
        if seeded:
            for ref, seed in zip((dw_ref, dbin_ref, vec_ref), refs[:3]):
                ref[...] = seed[...]
        else:
            dw_ref[...] = jnp.zeros_like(dw_ref)
            dbin_ref[...] = jnp.zeros_like(dbin_ref)
            vec_ref[...] = jnp.zeros_like(vec_ref)

    one16 = ones_row(n_lane * LANES)

    def row(i, carry):
        qs = [q_ref[t] for t in range(n_lane)]
        offs = [pl.multiple_of(q * LANES, LANES) for q in qs]
        fold = lambda val: sum(val[:, t * LANES:(t + 1) * LANES] for t in range(n_lane))
        z_rows = jnp.concatenate([z_ref[i, pl.ds(off, LANES), :] for off in offs], axis=0)
        x_hat, inv_std, znt = input_norm(z_rows, scale_ref[...], offset_ref[...])
        proj = dot_nn(w_ref[...], jnp.concatenate([znt, one16], axis=0))
        grad16 = []
        for g in range(chans // GROUP):
            parts = [proj[(4 * g + n) * GROUP:(4 * g + n + 1) * GROUP] for n in range(4)]
            vals = [None] * 4
            for n, ref in enumerate((da_ref, db_ref)):
                grad = jnp.concatenate([ref[i, g * GROUP:(g + 1) * GROUP, pl.ds(off, LANES)] for off in offs], axis=1).astype(F32)
                sig = jax.nn.sigmoid(parts[2 + n])
                vals[n] = grad * sig
                vals[2 + n] = vals[n] * parts[n] * (1.0 - sig)
            for n in range(4):
                dbin_ref[(4 * g + n) * GROUP:(4 * g + n + 1) * GROUP] += fold(vals[n])
                grad16.append(vals[n].astype(BF16))
        grad16 = jnp.concatenate(grad16, axis=0)
        gate = [g[i] for g in gls[:2]] + [g[i][:, part] for part in (slice(0, side), slice(side, LANES)) for g in gls[2:]]
        gate = jnp.concatenate(gate, axis=1)
        dw_ref[...] += dot_nt(znt, grad16)
        d_znorm = dot_nn(wb_ref[...], jnp.concatenate([grad16, gate], axis=0)).astype(BF16).astype(F32)
        vec_ref[0] += fold(d_znorm * x_hat)
        vec_ref[1] += fold(d_znorm)
        grad_hat = d_znorm * scale_ref[...]
        d_in = inv_std * (grad_hat - col_mean(grad_hat) - x_hat * col_mean(grad_hat * x_hat))
        d_rows = jnp.transpose(d_in)
        for t in range(n_lane):
            out = d_rows[t * LANES:(t + 1) * LANES] + dy_ref[i, pl.ds(offs[t], LANES), :].astype(F32)
            dz_ref[i, pl.ds(offs[t], LANES), :] = out.astype(BF16)
        return carry

    lax.fori_loop(0, ROWS, row, 0)


def final(q_all, z_rows, dy_rows, d_a, d_b, gates, w_t, w_back, scale, offset, first, d_z=None, seeds=()):
    _, n_col, chans = z_rows.shape
    n_step = d_b.shape[0] // ROWS
    at = first // ROWS
    full = lambda shape: pl.BlockSpec(shape, lambda s, q: (0,) * len(shape))
    pair_spec = pl.BlockSpec((ROWS, n_col, chans), lambda s, q: (s + at, 0, 0))
    sums = [(chans, 4 * chans), (4 * chans, LANES), (2, chans, LANES)]
    args = [q_all, z_rows, dy_rows, d_a, d_b, *gates, w_t, w_back, scale, offset, *seeds]
    in_specs = ([pair_spec, pair_spec, pl.BlockSpec((ROWS, chans, n_col), lambda s, q: (s + at, 0, 0)),
                 pl.BlockSpec((ROWS, chans, n_col), lambda s, q: (s, 0, 0))]
                + [pl.BlockSpec((ROWS, chans, LANES), lambda s, q: (s + at, 0, 0))] * 4
                + [full(w_t.shape), full(w_back.shape), full(scale.shape), full(offset.shape)]
                + [full(seed.shape) for seed in seeds])
    alias = {}
    if d_z is not None:
        alias = {len(args): 0}
        args.append(d_z)
        in_specs.append(pl.BlockSpec(memory_space=pl.ANY))
    return pl.pallas_call(
        functools.partial(final_kernel, bool(seeds)),
        grid_spec=pltpu.PrefetchScalarGridSpec(
            num_scalar_prefetch=1,
            grid=(n_step,),
            in_specs=in_specs,
            out_specs=[pair_spec] + [full(shape) for shape in sums],
        ),
        out_shape=[jax.ShapeDtypeStruct(z_rows.shape, BF16)] + [jax.ShapeDtypeStruct(shape, F32) for shape in sums],
        input_output_aliases=alias,
        compiler_params=pltpu.CompilerParams(vmem_limit_bytes=VMEM_LIMIT),
        cost_estimate=pl.CostEstimate(flops=30 * 10 ** 9, bytes_accessed=64 * 2 ** 20, transcendentals=0),
        name='final',
    )(*args)


def lane_bcast(vec, width):
    return jnp.broadcast_to(vec.astype(F32)[:, None], (vec.shape[0], width))


def local_step(z_loc, mask_loc, dy_loc, ln_in_scale, ln_in_offset, w_in, b_in, ln_out_scale, ln_out_offset, w_out, b_out, w_gate, b_gate):
    n_dap = lax.axis_size('dap')
    me = lax.axis_index('dap')
    swap = lambda arr, bit: lax.ppermute(arr, 'dap', [(d, d ^ bit) for d in range(n_dap)])
    w_t = with_bias(by_group(w_in).T, by_group(b_in))
    row_sc, row_of = (lane_bcast(v, z_loc.shape[1]) for v in (ln_in_scale, ln_in_offset))
    in_sc, in_of = lane_bcast(ln_in_scale, 256), lane_bcast(ln_in_offset, 256)
    out_sc, out_of = lane_bcast(ln_out_scale, 256), lane_bcast(ln_out_offset, 256)
    z_far = swap(z_loc, 2)
    rows = z_loc.shape[0]
    part = rows // 4
    mask_f = mask_loc.astype(F32)
    mask_loc = mask_loc.reshape(rows, -1, 1, LANES)
    mask_far = swap(mask_loc, 2)
    n_chunk = rows // part
    z_far = []
    for n in range(n_chunk):
        z_from = lax.optimization_barrier(z_loc) if n else z_loc
        z_far.append(swap(z_from[n * part:(n + 1) * part], 2))
    weights = (w_t, in_sc, in_of)
    a_0, b_0, zn = project(z_loc, mask_loc, 0, rows, *weights, True)
    b_1 = swap(b_0, 1)
    a_1 = swap(a_0, 1)
    blocks = [me ^ r for r in range(n_dap)]
    tail = (zn, dy_loc, with_bias(w_gate.T, b_gate), w_out, with_bias(w_out.T, b_out), out_sc, out_of)
    pieces = lambda *vals: jnp.stack(vals).astype(jnp.int32)
    mids = [middle(pieces(2 * blocks[0], 2 * blocks[0] + 1), a_0, [b_0], *tail)]
    mids.append(middle(pieces(2 * blocks[1], 2 * blocks[1] + 1), a_0, [b_1], *tail, after=(mids[0][5],)))
    near_out = [swap(mids[1][0], 1), swap(mids[1][1], 1)]
    a_2, b_2, a_3, b_3, far_out = [], [], [], [], []
    far_b = lambda h: b_2[2 * h:2 * h + 2] + b_3[2 * h:2 * h + 2]
    d_outs = lambda *tiles: [mids[t][n] for t in tiles for n in range(2)]
    order = (mids[1][5],)
    for h in range(2):
        for n in (2 * h, 2 * h + 1):
            a_n, b_n = project(z_far[n], mask_far, n * part, part, *weights, False, after=order)
            b_3.append(swap(b_n, 1))
            a_3.append(swap(a_n, 1))
            a_2.append(a_n)
            b_2.append(b_n)
            order = (a_n,)
            if n == 1:
                part_b = grad_sum(False, [mids[0][0], near_out[0], mids[0][1], near_out[1]], [a_0, a_1], mask_f, partial=True, after=order)
                order = (part_b,)
            if n == 2:
                part_a = grad_sum(True, d_outs(0, 1, 2), [b_0, b_1, *far_b(0)], mask_f, partial=True, after=order)
                order = (part_a,)
        mids.append(middle(pieces(2 * blocks[2] + h, 2 * blocks[3] + h), a_0, far_b(h), *tail, after=order))
        order = (mids[-1][5],)
        far_out.append([swap(mids[2 + h][0], 2), swap(mids[2 + h][1], 3)])
    d_a = grad_sum(True, d_outs(3), far_b(1), mask_f, seed=part_a)
    w_back = jnp.concatenate([by_group(w_in), w_gate], axis=1)
    d_z, seeds = None, ()
    for h in range(2):
        d_b = grad_sum(False, far_out[h], [*a_2, *a_3], mask_f, part=h, parts=2, seed=part_b, after=(d_a,) if h == 0 else (seeds[2],))
        d_z, *seeds = final(jnp.stack(blocks).astype(jnp.int32), z_loc, dy_loc, d_a, d_b, [m[2] for m in mids], w_t, w_back, row_sc, row_of,
                            h * (rows // 2), d_z, seeds)
    dw_t, dbin, vecs = seeds
    d_wo = sum(m[3] for m in mids)
    d_wg = sum(m[4] for m in mids).T
    vec_mid = jnp.sum(sum(m[5] for m in mids), axis=-1)
    vec_in = jnp.sum(vecs, axis=-1)
    summed = lax.psum((vec_in[0], vec_in[1], dw_t, jnp.sum(dbin, axis=-1), vec_mid[0], vec_mid[1], d_wo, vec_mid[2], d_wg, vec_mid[3]), 'dap')
    summed = list(summed)
    summed[2] = from_group(summed[2])
    summed[3] = from_group(summed[3])
    return (d_z,) + tuple(piece.astype(BF16) for piece in summed)


def solution(mesh):
    pair_spec = P(('batch', 'dap'), None, None)
    mask_spec = P(('batch', 'dap'), None)
    vec_rep = P(None)
    mat_rep = P(None, None)
    vec_part = P('batch')
    mat_part = P('batch', None)
    in_specs = (pair_spec, mask_spec, pair_spec, vec_rep, vec_rep, mat_rep, vec_rep, vec_rep, vec_rep, mat_rep, vec_rep, mat_rep, vec_rep)
    out_specs = (pair_spec, vec_part, vec_part, mat_part, vec_part, vec_part, vec_part, mat_part, vec_part, mat_part, vec_part)
    return jax.shard_map(local_step, mesh=mesh, in_specs=in_specs, out_specs=out_specs, check_vma=False)
```

profile of v0, /device:TPU:0, one launch (start us, length us, event | category | flops | bytes accessed | tf_op | source)
XLA Modules:
  0.0 805.4 jit_solution(14332016841715952819)
XLA Ops:
  0.6 2.0 reshape.48.mask_ref
  6.0 1.4 broadcast_in_dim.19.scale_ref
  7.4 1.4 broadcast_in_dim.20.offset_ref
  8.8 72.5 %project.5 = (bf16[128,128,512]{2,1,0:T(8,128)(2,1)}, bf16[128,128,512]{2,1,0:T(8,128)(2,1)}, bf16[128,512,128]{2,1,0:T(8,128)(2,1)}) custom-call(bf16[128,512,128]{2,1,0:T(8,128)(2,1)} %z_ref.5, s32[128,4,1,128]{3,2,1,0:T(1,128)} %reshape.48.mask_ref, bf16[512,256]{1,0:T(8,128)(2,1)} %maximum_maximum_fusion.w_ref, f32[128,256]{1,0:T(8,128)} %broadcast_in_dim.19.scale_ref, ...), custom_call_target="tpu_custom_call" | custom-call | flops 25600000000 | bytes 67108864 | tf_op jit(solution)/shard_map/project/pallas_call | solution.py:115
  82.1 3.0 collective-permute-start.1
  85.1 4.6 slice.31
  89.8 9.0 %fusion = (bf16[32,512,128]{2,1,0:T(8,128)(2,1)}, bf16[32,512,128]{2,1,0:T(8,128)(2,1)}, bf16[32,512,128]{2,1,0:T(8,128)(2,1)}) fusion(bf16[128,512,128]{2,1,0:T(8,128)(2,1)} %z_ref.5), kind=kLoop, calls=%fused_computation.18 | loop fusion | bytes 25165824 | tf_op jit(solution)/shard_map/slice | solution.py:428
  98.8 2.0 collective-permute-start.4
  104.7 49.6 %middle.4 = (bf16[128,64,128]{2,1,0:T(8,128)(2,1)}, bf16[128,64,128]{2,1,0:T(8,128)(2,1)}, bf16[128,128,128]{2,1,0:T(8,128)(2,1)}, f32[128,128]{1,0:T(8,128)}, f...) custom-call(s32[2]{0:T(128)} %pad_add_fusion.4.idx_ref, bf16[128,128,512]{2,1,0:T(8,128)(2,1)} %get-tuple-element.54.a_ref.refs_4_, ...), custom_call_target="tpu_custom_call" | custom-call | flops 24999999488 | bytes 50331648 | tf_op jit(solution)/shard_map/middle/pallas_call | solution.py:216
  154.3 49.6 %middle.5 = (bf16[128,64,128]{2,1,0:T(8,128)(2,1)}, bf16[128,64,128]{2,1,0:T(8,128)(2,1)}, bf16[128,128,128]{2,1,0:T(8,128)(2,1)}, f32[128,128]{1,0:T(8,128)}, f...) custom-call(s32[2]{0:T(128)} %pad_add_fusion.3.idx_ref, bf16[128,128,512]{2,1,0:T(8,128)(2,1)} %get-tuple-element.54.a_ref.refs_4_, ...), custom_call_target="tpu_custom_call" | custom-call | flops 24999999488 | bytes 50331648 | tf_op jit(solution)/shard_map/middle/pallas_call | solution.py:216
  204.7 20.6 %project.6 = (bf16[128,32,512]{2,1,0:T(8,128)(2,1)}, bf16[128,32,512]{2,1,0:T(8,128)(2,1)}) custom-call(bf16[32,512,128]{2,1,0:T(8,128)(2,1)} %collective-permute-done.2.z_ref, s32[128,4,1,128]{3,2,1,0:T(1,128)} %copy-done.7, bf16[512,256]{1,0:T(8,128)(2,1)} %maximum_maximum_fusion.w_ref, f32[128,256]{1,0:T(8,128)} %broadcast_in_dim.19.scale_ref, ...), custom_call_target="tpu_custom_call" | custom-call | flops 6400000000 | bytes 16777216 | tf_op jit(solution)/shard_map/project/pallas_call | solution.py:115
  225.3 46.9 %collective-permute-done.4.z_ref = bf16[32,512,128]{2,1,0:T(8,128)(2,1)} collective-permute-done((bf16[32,512,128]{2,1,0:T(8,128)(2,1)}, bf16[32,512,128]{2,1,0:T(8,128)(2,1)}, u32[]{:S(2)}, u32[]{:S(2)}) %collective-permute-start.4) | collective-permute-done | bytes 4194336 | tf_op jit(solution)/shard_map/ppermute | solution.py:413
  272.2 20.7 %project.7 = (bf16[128,32,512]{2,1,0:T(8,128)(2,1)}, bf16[128,32,512]{2,1,0:T(8,128)(2,1)}) custom-call(bf16[32,512,128]{2,1,0:T(8,128)(2,1)} %collective-permute-done.4.z_ref, s32[128,4,1,128]{3,2,1,0:T(1,128)} %copy-done.7, bf16[512,256]{1,0:T(8,128)(2,1)} %maximum_maximum_fusion.w_ref, f32[128,256]{1,0:T(8,128)} %broadcast_in_dim.19.scale_ref, ...), custom_call_target="tpu_custom_call" | custom-call | flops 6400000000 | bytes 16777216 | tf_op jit(solution)/shard_map/project/pallas_call | solution.py:115
  295.0 8.3 %collective-permute-done.7.refs_1_ = bf16[128,64,128]{2,1,0:T(8,128)(2,1)} collective-permute-done((bf16[128,64,128]{2,1,0:T(8,128)(2,1)S(1)}, bf16[128,64,128]{2,1,0:T(8,128)(2,1)}, u32[]{:S(2)}, u32[]{:S(2)}) %collective-permute-start.7) | collective-permute-done | bytes 2097184 | tf_op jit(solution)/shard_map/ppermute | solution.py:413
  304.4 2.0 collective-permute-done.8.refs_3_
  306.5 27.5 %shard_map.212.refs_13_.refs_10_ = f32[128,128,512]{2,1,0:T(8,128)} custom-call(bf16[128,64,128]{2,1,0:T(8,128)(2,1)} %get-tuple-element.62.refs_0_, bf16[128,64,128]{2,1,0:T(8,128)(2,1)} %collective-permute-done.7.refs_1_, bf16[128,64,128]{2,1,0:T(8,128)(2,1)} %get-tuple-element.64.refs_2_.refs_1_, bf16[128,64,128]{2,1,0:T(8,128)(2,1)} %collective-permute-done.8.refs_3_, ...), custom_call_target="tpu_custom_call" | custom-call | flops 12000000000 | bytes 83886080 | tf_op jit(solution)/shard_map/pallas_call | solution.py:303
  334.0 49.3 %middle.6 = (bf16[128,64,128]{2,1,0:T(8,128)(2,1)}, bf16[128,64,128]{2,1,0:T(8,128)(2,1)}, bf16[128,128,128]{2,1,0:T(8,128)(2,1)}, f32[128,128]{1,0:T(8,128)}, f...) custom-call(s32[2]{0:T(128)} %pad_add_fusion.2.idx_ref, bf16[128,128,512]{2,1,0:T(8,128)(2,1)} %get-tuple-element.54.a_ref.refs_4_, ...), custom_call_target="tpu_custom_call" | custom-call | flops 24999999488 | bytes 50331648 | tf_op jit(solution)/shard_map/middle/pallas_call | solution.py:216
  383.3 3.9 collective-permute-done.z_ref
  387.2 20.5 %project.8 = (bf16[128,32,512]{2,1,0:T(8,128)(2,1)}, bf16[128,32,512]{2,1,0:T(8,128)(2,1)}) custom-call(bf16[32,512,128]{2,1,0:T(8,128)(2,1)} %collective-permute-done.z_ref, s32[128,4,1,128]{3,2,1,0:T(1,128)} %copy-done.7, bf16[512,256]{1,0:T(8,128)(2,1)} %maximum_maximum_fusion.w_ref, f32[128,256]{1,0:T(8,128)} %broadcast_in_dim.19.scale_ref, ...), custom_call_target="tpu_custom_call" | custom-call | flops 6400000000 | bytes 16777216 | tf_op jit(solution)/shard_map/project/pallas_call | solution.py:115
  407.7 33.7 %shard_map.213.refs_0_.refs_6_ = f32[128,128,512]{2,1,0:T(8,128)} custom-call(bf16[128,64,128]{2,1,0:T(8,128)(2,1)} %get-tuple-element.62.refs_0_, bf16[128,64,128]{2,1,0:T(8,128)(2,1)} %get-tuple-element.64.refs_2_.refs_1_, bf16[128,64,128]{2,1,0:T(8,128)(2,1)} %get-tuple-element.63.refs_2_, bf16[128,64,128]{2,1,0:T(8,128)(2,1)} %get-tuple-element.65.refs_3_, ...), custom_call_target="tpu_custom_call" | custom-call | flops 12000000000 | bytes 83886080 | tf_op jit(solution)/shard_map/pallas_call | solution.py:303
  441.5 35.1 %collective-permute-done.10.z_ref = bf16[32,512,128]{2,1,0:T(8,128)(2,1)} collective-permute-done((bf16[32,512,128]{2,1,0:T(8,128)(2,1)}, bf16[32,512,128]{2,1,0:T(8,128)(2,1)}, u32[]{:S(2)}, u32[]{:S(2)}) %collective-permute-start.10) | collective-permute-done | bytes 4194336 | tf_op jit(solution)/shard_map/ppermute | solution.py:413
  476.6 20.5 %project.9 = (bf16[128,32,512]{2,1,0:T(8,128)(2,1)}, bf16[128,32,512]{2,1,0:T(8,128)(2,1)}) custom-call(bf16[32,512,128]{2,1,0:T(8,128)(2,1)} %collective-permute-done.10.z_ref, s32[128,4,1,128]{3,2,1,0:T(1,128)} %copy-done.7, bf16[512,256]{1,0:T(8,128)(2,1)} %maximum_maximum_fusion.w_ref, f32[128,256]{1,0:T(8,128)} %broadcast_in_dim.19.scale_ref, ...), custom_call_target="tpu_custom_call" | custom-call | flops 6400000000 | bytes 16777216 | tf_op jit(solution)/shard_map/project/pallas_call | solution.py:115
  502.0 2.6 collective-permute-done.12.refs_3_.refs_5_
  505.4 49.2 %middle.7 = (bf16[128,64,128]{2,1,0:T(8,128)(2,1)}, bf16[128,64,128]{2,1,0:T(8,128)(2,1)}, bf16[128,128,128]{2,1,0:T(8,128)(2,1)}, f32[128,128]{1,0:T(8,128)}, f...) custom-call(s32[2]{0:T(128)} %pad_add_fusion.1.idx_ref, bf16[128,128,512]{2,1,0:T(8,128)(2,1)} %get-tuple-element.54.a_ref.refs_4_, ...), custom_call_target="tpu_custom_call" | custom-call | flops 24999999488 | bytes 50331648 | tf_op jit(solution)/shard_map/middle/pallas_call | solution.py:216
  554.6 1.1 add_reduce_fusion
  556.7 27.0 %shard_map.214.refs_12_.da_ref = bf16[128,128,512]{2,1,0:T(8,128)(2,1)} custom-call(bf16[128,64,128]{2,1,0:T(8,128)(2,1)} %get-tuple-element.74.refs_0_, bf16[128,64,128]{2,1,0:T(8,128)(2,1)} %get-tuple-element.75.refs_1_, bf16[128,32,512]{2,1,0:T(8,128)(2,1)} %get-tuple-element.68.refs_0_.refs_2_, bf16[128,32,512]{2,1,0:T(8,128)(2,1)} %get-tuple-element.72.refs_1_.refs_3_, ...), custom_call_target="tpu_custom_call" | custom-call | flops 12000000000 | bytes 83886080 | tf_op jit(solution)/shard_map/pallas_call | solution.py:303
  585.4 7.7 collective-permute-done.20.refs_1_
  593.2 23.3 %shard_map.215.db_ref = bf16[64,128,512]{2,1,0:T(8,128)(2,1)} custom-call(bf16[128,64,128]{2,1,0:T(8,128)(2,1)} %collective-permute-done.19.refs_0_, bf16[128,64,128]{2,1,0:T(8,128)(2,1)} %collective-permute-done.20.refs_1_, bf16[128,32,512]{2,1,0:T(8,128)(2,1)} %get-tuple-element.60.refs_0_.refs_2_, ...), custom_call_target="tpu_custom_call" | custom-call | flops 12000000000 | bytes 83886080 | tf_op jit(solution)/shard_map/pallas_call | solution.py:303
  618.0 70.6 %final.2 = (bf16[128,512,128]{2,1,0:T(8,128)(2,1)}, f32[128,512]{1,0:T(8,128)}, f32[512,128]{1,0:T(8,128)}, f32[2,128,128]{2,1,0:T(8,128)}) custom-call(s32[4]{0:T(128)} %pad_add_fusion.q_ref, bf16[128,512,128]{2,1,0:T(8,128)(2,1)} %z_ref.5, bf16[128,512,128]{2,1,0:T(8,128)(2,1)} %dy_ref.3, bf16[128,128,512]{2,1,0:T(8,128)(2,1)} %shard_map.214.refs_12_.da_ref, ...), custom_call_target="tpu_custom_call" | custom-call | flops 30000001024 | bytes 67108864 | tf_op jit(solution)/shard_map/final/pallas_call | solution.py:390
  688.7 23.3 %shard_map.216.db_ref = bf16[64,128,512]{2,1,0:T(8,128)(2,1)} custom-call(bf16[128,64,128]{2,1,0:T(8,128)(2,1)} %collective-permute-done.13.refs_0_, bf16[128,64,128]{2,1,0:T(8,128)(2,1)} %collective-permute-done.14.refs_1_, bf16[128,32,512]{2,1,0:T(8,128)(2,1)} %get-tuple-element.60.refs_0_.refs_2_, ...), custom_call_target="tpu_custom_call" | custom-call | flops 12000000000 | bytes 83886080 | tf_op jit(solution)/shard_map/pallas_call | solution.py:303
  711.9 70.8 %final.3 = (bf16[128,512,128]{2,1,0:T(8,128)(2,1)}, f32[128,512]{1,0:T(8,128)}, f32[512,128]{1,0:T(8,128)}, f32[2,128,128]{2,1,0:T(8,128)}) custom-call(s32[4]{0:T(128)} %pad_add_fusion.q_ref, bf16[128,512,128]{2,1,0:T(8,128)(2,1)} %z_ref.5, bf16[128,512,128]{2,1,0:T(8,128)(2,1)} %dy_ref.3, ...), custom_call_target="tpu_custom_call", output_to_operand_aliasing={{0}: (16, {})} | custom-call | flops 30000001024 | bytes 67108864 | tf_op jit(solution)/shard_map/final/pallas_call | solution.py:390
  784.9 18.1 %all-reduce.2 = (bf16[128]{0:T(256)(128)(2,1)}, bf16[128]{0:T(256)(128)(2,1)}, bf16[128,512]{1,0:T(8,128)(2,1)S(1)}, bf16[512]{0:T(512)(128)(2,1)S(1)}, bf16[128...) all-reduce(f32[128]{0:T(128)S(1)} %get-tuple-element.148, ...), channel_id=1, replica_groups=mesh['batch'=2,'dap'=4] {'dap'}, use_global_device_ids=true, to_apply=%region_1.0 | all-reduce | flops 99584 | bytes 597504 | tf_op jit(solution)/shard_map/psum | solution.py:472
  (120 shorter events, 26.5 us)
Async XLA Ops:
  8.8 73.3 %copy-start.8 = (s32[128,4,1,128]{3,2,1,0:T(1,128)S(1)}, s32[128,4,1,128]{3,2,1,0:T(1,128)}, u32[]{:S(2)}) copy-start(s32[128,4,1,128]{3,2,1,0:T(1,128)} %reshape.48.mask_ref) | copy-start | bytes 786436
  81.3 73.1 %collective-permute-start.3 = (bf16[128,128,512]{2,1,0:T(8,128)(2,1)}, bf16[128,128,512]{2,1,0:T(8,128)(2,1)}, u32[]{:S(2)}, u32[]{:S(2)}) collective-permute-start(bf16[128,128,512]{2,1,0:T(8,128)(2,1)} %get-tuple-element.55.refs_0_.refs_6_), channel_id=1, source_target_pairs={{0,1},{1,0},{2,3},{3,2},{4,5},{5,4},{6,7},{7,6}} | collective-permute-start | bytes 50331656 | tf_op jit(solution)/shard_map/ppermute | solution.py:413
  82.1 211.3 %collective-permute-start.9 = (bf16[128,128,512]{2,1,0:T(8,128)(2,1)}, bf16[128,128,512]{2,1,0:T(8,128)(2,1)}, u32[]{:S(2)}, u32[]{:S(2)}) collective-permute-start(bf16[128,128,512]{2,1,0:T(8,128)(2,1)} %get-tuple-element.54.a_ref.refs_4_), channel_id=1, source_target_pairs={{0,1},{1,0},{2,3},{3,2},{4,5},{5,4},{6,7},{7,6}} | collective-permute-start | bytes 50331656 | tf_op jit(solution)/shard_map/ppermute | solution.py:413
  82.1 121.8 %collective-permute-start.1 = (s32[128,4,1,128]{3,2,1,0:T(1,128)S(1)}, s32[128,4,1,128]{3,2,1,0:T(1,128)S(1)}, u32[]{:S(2)}, u32[]{:S(2)}) collective-permute-start(s32[128,4,1,128]{3,2,1,0:T(1,128)S(1)} %copy-done.8), channel_id=1, source_target_pairs={{0,2},{1,3},{2,0},{3,1},{4,6},{5,7},{6,4},{7,5}} | collective-permute-start | bytes 786440 | tf_op jit(solution)/shard_map/ppermute | solution.py:413
  89.8 114.2 %collective-permute-start.2 = (bf16[32,512,128]{2,1,0:T(8,128)(2,1)}, bf16[32,512,128]{2,1,0:T(8,128)(2,1)}, u32[]{:S(2)}, u32[]{:S(2)}) collective-permute-start(bf16[32,512,128]{2,1,0:T(8,128)(2,1)} %slice.31), channel_id=1, source_target_pairs={{0,2},{1,3},{2,0},{3,1},{4,6},{5,7},{6,4},{7,5}} | collective-permute-start | bytes 12582920 | tf_op jit(solution)/shard_map/ppermute | solution.py:413
  98.8 173.4 %collective-permute-start.4 = (bf16[32,512,128]{2,1,0:T(8,128)(2,1)}, bf16[32,512,128]{2,1,0:T(8,128)(2,1)}, u32[]{:S(2)}, u32[]{:S(2)}) collective-permute-start(bf16[32,512,128]{2,1,0:T(8,128)(2,1)} %get-tuple-element.141), channel_id=1, source_target_pairs={{0,2},{1,3},{2,0},{3,1},{4,6},{5,7},{6,4},{7,5}} | collective-permute-start | bytes 12582920 | tf_op jit(solution)/shard_map/ppermute | solution.py:413
  225.2 108.7 %collective-permute-start.5 = (bf16[128,32,512]{2,1,0:T(8,128)(2,1)}, bf16[128,32,512]{2,1,0:T(8,128)(2,1)}, u32[]{:S(2)}, u32[]{:S(2)}) collective-permute-start(bf16[128,32,512]{2,1,0:T(8,128)(2,1)} %get-tuple-element.59.refs_0_.refs_8_), channel_id=1, source_target_pairs={{0,1},{1,0},{2,3},{3,2},{4,5},{5,4},{6,7},{7,6}} | collective-permute-start | bytes 12582920 | tf_op jit(solution)/shard_map/ppermute | solution.py:413
  292.9 41.1 %collective-permute-start.6 = (bf16[128,32,512]{2,1,0:T(8,128)(2,1)}, bf16[128,32,512]{2,1,0:T(8,128)(2,1)}, u32[]{:S(2)}, u32[]{:S(2)}) collective-permute-start(bf16[128,32,512]{2,1,0:T(8,128)(2,1)} %get-tuple-element.61.refs_1_.refs_9_), channel_id=1, source_target_pairs={{0,1},{1,0},{2,3},{3,2},{4,5},{5,4},{6,7},{7,6}} | collective-permute-start | bytes 12582920 | tf_op jit(solution)/shard_map/ppermute | solution.py:413
  292.9 10.5 %collective-permute-start.7 = (bf16[128,64,128]{2,1,0:T(8,128)(2,1)S(1)}, bf16[128,64,128]{2,1,0:T(8,128)(2,1)}, u32[]{:S(2)}, u32[]{:S(2)}) collective-permute-start(bf16[128,64,128]{2,1,0:T(8,128)(2,1)S(1)} %copy-done.1), channel_id=1, source_target_pairs={{0,1},{1,0},{2,3},{3,2},{4,5},{5,4},{6,7},{7,6}} | collective-permute-start | bytes 6291464 | tf_op jit(solution)/shard_map/ppermute | solution.py:413
  293.4 13.0 %collective-permute-start.8 = (bf16[128,64,128]{2,1,0:T(8,128)(2,1)}, bf16[128,64,128]{2,1,0:T(8,128)(2,1)}, u32[]{:S(2)}, u32[]{:S(2)}) collective-permute-start(bf16[128,64,128]{2,1,0:T(8,128)(2,1)} %get-tuple-element.65.refs_3_), channel_id=1, source_target_pairs={{0,1},{1,0},{2,3},{3,2},{4,5},{5,4},{6,7},{7,6}} | collective-permute-start | bytes 6291464 | tf_op jit(solution)/shard_map/ppermute | solution.py:413
  293.4 93.8 %collective-permute-start = (bf16[32,512,128]{2,1,0:T(8,128)(2,1)}, bf16[32,512,128]{2,1,0:T(8,128)(2,1)}, u32[]{:S(2)}, u32[]{:S(2)}) collective-permute-start(bf16[32,512,128]{2,1,0:T(8,128)(2,1)} %get-tuple-element.142), channel_id=1, source_target_pairs={{0,2},{1,3},{2,0},{3,1},{4,6},{5,7},{6,4},{7,5}} | collective-permute-start | bytes 12582920 | tf_op jit(solution)/shard_map/ppermute | solution.py:413
  303.4 173.2 %collective-permute-start.10 = (bf16[32,512,128]{2,1,0:T(8,128)(2,1)}, bf16[32,512,128]{2,1,0:T(8,128)(2,1)}, u32[]{:S(2)}, u32[]{:S(2)}) collective-permute-start(bf16[32,512,128]{2,1,0:T(8,128)(2,1)} %get-tuple-element.140), channel_id=1, source_target_pairs={{0,2},{1,3},{2,0},{3,1},{4,6},{5,7},{6,4},{7,5}} | collective-permute-start | bytes 12582920 | tf_op jit(solution)/shard_map/ppermute | solution.py:413
  306.4 193.4 %collective-permute-start.15 = (bf16[128,32,512]{2,1,0:T(8,128)(2,1)}, bf16[128,32,512]{2,1,0:T(8,128)(2,1)}, u32[]{:S(2)}, u32[]{:S(2)}) collective-permute-start(bf16[128,32,512]{2,1,0:T(8,128)(2,1)} %get-tuple-element.60.refs_0_.refs_2_), channel_id=1, source_target_pairs={{0,1},{1,0},{2,3},{3,2},{4,5},{5,4},{6,7},{7,6}} | collective-permute-start | bytes 12582920 | tf_op jit(solution)/shard_map/ppermute | solution.py:413
  407.7 93.2 %collective-permute-start.11 = (bf16[128,32,512]{2,1,0:T(8,128)(2,1)}, bf16[128,32,512]{2,1,0:T(8,128)(2,1)}, u32[]{:S(2)}, u32[]{:S(2)}) collective-permute-start(bf16[128,32,512]{2,1,0:T(8,128)(2,1)} %get-tuple-element.68.refs_0_.refs_2_), channel_id=1, source_target_pairs={{0,1},{1,0},{2,3},{3,2},{4,5},{5,4},{6,7},{7,6}} | collective-permute-start | bytes 12582920 | tf_op jit(solution)/shard_map/ppermute | solution.py:413
  441.5 55.7 %copy-start.5 = (s32[128,512]{1,0:T(8,128)S(1)}, s32[128,512]{1,0:T(8,128)}, u32[]{:S(2)}) copy-start(s32[128,512]{1,0:T(8,128)} %param.14) | copy-start | bytes 786436
  441.5 56.4 %copy-start.3 = (bf16[128,8,4,16]{0,3,2,1:T(8,128)(2,1)S(1)}, bf16[128,8,4,16]{0,3,2,1:T(8,128)(2,1)}, u32[]{:S(2)}) copy-start(bf16[128,8,4,16]{0,3,2,1:T(8,128)(2,1)} %copy-done.2) | copy-start | bytes 393220
  441.5 57.1 %copy-start.12 = (bf16[128,128]{1,0:T(8,128)(2,1)S(1)}, bf16[128,128]{1,0:T(8,128)(2,1)}, u32[]{:S(2)}) copy-start(bf16[128,128]{1,0:T(8,128)(2,1)} %param.24) | copy-start | bytes 98308
  441.5 63.1 %copy-start = (bf16[128,64,128]{2,1,0:T(8,128)(2,1)S(1)}, bf16[128,64,128]{2,1,0:T(8,128)(2,1)}, u32[]{:S(2)}) copy-start(bf16[128,64,128]{2,1,0:T(8,128)(2,1)} %get-tuple-element.70.refs_5_) | copy-start | bytes 6291460
  497.1 7.5 collective-permute-start.12
  499.3 84.4 %collective-permute-start.16 = (bf16[128,32,512]{2,1,0:T(8,128)(2,1)}, bf16[128,32,512]{2,1,0:T(8,128)(2,1)}, u32[]{:S(2)}, u32[]{:S(2)}) collective-permute-start(bf16[128,32,512]{2,1,0:T(8,128)(2,1)} %get-tuple-element.66.refs_6_.refs_3_), channel_id=1, source_target_pairs={{0,1},{1,0},{2,3},{3,2},{4,5},{5,4},{6,7},{7,6}} | collective-permute-start | bytes 12582920 | tf_op jit(solution)/shard_map/ppermute | solution.py:413
  499.8 93.4 %collective-permute-start.17 = (bf16[128,32,512]{2,1,0:T(8,128)(2,1)}, bf16[128,32,512]{2,1,0:T(8,128)(2,1)}, u32[]{:S(2)}, u32[]{:S(2)}) collective-permute-start(bf16[128,32,512]{2,1,0:T(8,128)(2,1)} %get-tuple-element.71.refs_12_.refs_4_), channel_id=1, source_target_pairs={{0,1},{1,0},{2,3},{3,2},{4,5},{5,4},{6,7},{7,6}} | collective-permute-start | bytes 12582920 | tf_op jit(solution)/shard_map/ppermute | solution.py:413
  499.8 93.4 %collective-permute-start.18 = (bf16[128,32,512]{2,1,0:T(8,128)(2,1)}, bf16[128,32,512]{2,1,0:T(8,128)(2,1)}, u32[]{:S(2)}, u32[]{:S(2)}) collective-permute-start(bf16[128,32,512]{2,1,0:T(8,128)(2,1)} %get-tuple-element.73.refs_13_.refs_5_), channel_id=1, source_target_pairs={{0,1},{1,0},{2,3},{3,2},{4,5},{5,4},{6,7},{7,6}} | collective-permute-start | bytes 12582920 | tf_op jit(solution)/shard_map/ppermute | solution.py:413
  500.9 54.8 %copy-start.13 = (f32[128,128]{1,0:T(8,128)S(1)}, f32[128,128]{1,0:T(8,128)}, u32[]{:S(2)}) copy-start(f32[128,128]{1,0:T(8,128)} %get-tuple-element.89) | copy-start | bytes 196612
  500.9 54.8 %copy-start.14 = (f32[128,128]{1,0:T(8,128)S(1)}, f32[128,128]{1,0:T(8,128)}, u32[]{:S(2)}) copy-start(f32[128,128]{1,0:T(8,128)} %get-tuple-element.93) | copy-start | bytes 196612
  500.9 54.8 %copy-start.15 = (f32[128,128]{1,0:T(8,128)S(1)}, f32[128,128]{1,0:T(8,128)}, u32[]{:S(2)}) copy-start(f32[128,128]{1,0:T(8,128)} %get-tuple-element.90) | copy-start | bytes 196612
  500.9 54.8 %copy-start.16 = (f32[128,128]{1,0:T(8,128)S(1)}, f32[128,128]{1,0:T(8,128)}, u32[]{:S(2)}) copy-start(f32[128,128]{1,0:T(8,128)} %get-tuple-element.94) | copy-start | bytes 196612
  500.9 54.8 %copy-start.17 = (f32[128,128]{1,0:T(8,128)S(1)}, f32[128,128]{1,0:T(8,128)}, u32[]{:S(2)}) copy-start(f32[128,128]{1,0:T(8,128)} %get-tuple-element.91) | copy-start | bytes 196612
  500.9 54.8 %copy-start.18 = (f32[128,128]{1,0:T(8,128)S(1)}, f32[128,128]{1,0:T(8,128)}, u32[]{:S(2)}) copy-start(f32[128,128]{1,0:T(8,128)} %get-tuple-element.95) | copy-start | bytes 196612
  500.9 83.8 %collective-permute-start.19 = (bf16[128,64,128]{2,1,0:T(8,128)(2,1)}, bf16[128,64,128]{2,1,0:T(8,128)(2,1)}, u32[]{:S(2)}, u32[]{:S(2)}) collective-permute-start(bf16[128,64,128]{2,1,0:T(8,128)(2,1)} %get-tuple-element.69.refs_4_), channel_id=1, source_target_pairs={{0,2},{1,3},{2,0},{3,1},{4,6},{5,7},{6,4},{7,5}} | collective-permute-start | bytes 6291464 | tf_op jit(solution)/shard_map/ppermute | solution.py:413
  504.6 88.5 %collective-permute-start.20 = (bf16[128,64,128]{2,1,0:T(8,128)(2,1)S(1)}, bf16[128,64,128]{2,1,0:T(8,128)(2,1)}, u32[]{:S(2)}, u32[]{:S(2)}) collective-permute-start(bf16[128,64,128]{2,1,0:T(8,128)(2,1)S(1)} %copy-done), channel_id=1, source_target_pairs={{0,3},{1,2},{2,1},{3,0},{4,7},{5,6},{6,5},{7,4}} | collective-permute-start | bytes 6291464 | tf_op jit(solution)/shard_map/ppermute | solution.py:413
  583.7 105.0 %collective-permute-start.13 = (bf16[128,64,128]{2,1,0:T(8,128)(2,1)}, bf16[128,64,128]{2,1,0:T(8,128)(2,1)}, u32[]{:S(2)}, u32[]{:S(2)}) collective-permute-start(bf16[128,64,128]{2,1,0:T(8,128)(2,1)} %get-tuple-element.74.refs_0_), channel_id=1, source_target_pairs={{0,2},{1,3},{2,0},{3,1},{4,6},{5,7},{6,4},{7,5}} | collective-permute-start | bytes 6291464 | tf_op jit(solution)/shard_map/ppermute | solution.py:413
  584.7 104.0 %collective-permute-start.14 = (bf16[128,64,128]{2,1,0:T(8,128)(2,1)}, bf16[128,64,128]{2,1,0:T(8,128)(2,1)}, u32[]{:S(2)}, u32[]{:S(2)}) collective-permute-start(bf16[128,64,128]{2,1,0:T(8,128)(2,1)} %get-tuple-element.75.refs_1_), channel_id=1, source_target_pairs={{0,3},{1,2},{2,1},{3,0},{4,7},{5,6},{6,5},{7,4}} | collective-permute-start | bytes 6291464 | tf_op jit(solution)/shard_map/ppermute | solution.py:413
  (14 other events, 322.4 us)
where the time goes:
time: 806 us; the launch traced here: 805 us
  Pallas kernels  629 us (78%)
  waiting for transfers between devices  107 us (13%)
  local copies, waits for them, and re-layouts  27.8 us (3%)
  blocking collectives  18.1 us (2%)
  starting transfers between devices  13.1 us (2%)
  other arithmetic  9.94 us (1%)
    pallas_call x4, Pallas kernels, middle(): pl.pallas_call(functools.partial(middle_kernel, n_mul, n_mid, len(b_parts...  198 us
    pallas_call x5, Pallas kernels, project(): pl.pallas_call(functools.partial(project_kernel, keep_norm), grid=(rows /...  155 us
    pallas_call x2, Pallas kernels, final(): pl.pallas_call(functools.partial(final_kernel, bool(seeds)), grid_spec=pl...  141 us
    pallas_call x5, Pallas kernels, grad_sum(): pl.pallas_call(functools.partial(grad_kernel, trans, len(grads), len(acts...  135 us
    ppermute x21, waiting for transfers between devices, local_step(): lax.ppermute(arr, 'dap', [(d, d ^ bit) for d in range(n_dap)])  107 us
    psum x1, blocking collectives, local_step(): lax.psum((vec_in[0], vec_in[1], dw_t, jnp.sum(dbin, axis=-1), vec_mid[0],...  18.1 us
  transfers between devices with their start and end apart: 21, of which 7 were waited for; matrix products, arithmetic and copies ran while one was open for 3% of the time, Pallas kernels for 57%

commit v1 on v0

--- a/solution.py
+++ b/solution.py
@@ -86,7 +86,7 @@
                         scr[pl.ds(at, GROUP, stride=pitch), :] = val[:, t * LANES:(t + 1) * LANES]
         return carry
 
-    lax.fori_loop(0, ROWS, row, 0)
+    lax.fori_loop(0, ROWS, row, 0, unroll=2)
 
     def pack(c, carry):
         for t in range(n_lane):
@@ -188,7 +188,7 @@
             dwg_ref[...] += dot_nn(gate16, zn)
             return carry
 
-        lax.fori_loop(0, MID_ROWS // 2, pair, 0)
+        lax.fori_loop(0, MID_ROWS // 2, pair, 0, unroll=2)
 
     @pl.when(step >= n_mul + n_mid)
     def _():
@@ -354,7 +354,7 @@
         grad16 = jnp.concatenate(grad16, axis=0)
         gate = [g[i] for g in gls[:2]] + [g[i][:, part] for part in (slice(0, side), slice(side, LANES)) for g in gls[2:]]
         gate = jnp.concatenate(gate, axis=1)
-        dw_ref[...] += dot_nt(znt, grad16)
+        dw_ref[...] += dot_nn(grad16, jnp.transpose(znt))
         d_znorm = dot_nn(wb_ref[...], jnp.concatenate([grad16, gate], axis=0)).astype(BF16).astype(F32)
         vec_ref[0] += fold(d_znorm * x_hat)
         vec_ref[1] += fold(d_znorm)
@@ -366,7 +366,7 @@
             dz_ref[i, pl.ds(offs[t], LANES), :] = out.astype(BF16)
         return carry
 
-    lax.fori_loop(0, ROWS, row, 0)
+    lax.fori_loop(0, ROWS, row, 0, unroll=2)
 
 
 def final(q_all, z_rows, dy_rows, d_a, d_b, gates, w_t, w_back, scale, offset, first, d_z=None, seeds=()):
@@ -375,7 +375,7 @@
     at = first // ROWS
     full = lambda shape: pl.BlockSpec(shape, lambda s, q: (0,) * len(shape))
     pair_spec = pl.BlockSpec((ROWS, n_col, chans), lambda s, q: (s + at, 0, 0))
-    sums = [(chans, 4 * chans), (4 * chans, LANES), (2, chans, LANES)]
+    sums = [(4 * chans, chans), (4 * chans, LANES), (2, chans, LANES)]
     args = [q_all, z_rows, dy_rows, d_a, d_b, *gates, w_t, w_back, scale, offset, *seeds]
     in_specs = ([pair_spec, pair_spec, pl.BlockSpec((ROWS, chans, n_col), lambda s, q: (s + at, 0, 0)),
                  pl.BlockSpec((ROWS, chans, n_col), lambda s, q: (s, 0, 0))]
@@ -471,7 +471,7 @@
     vec_in = jnp.sum(vecs, axis=-1)
     summed = lax.psum((vec_in[0], vec_in[1], dw_t, jnp.sum(dbin, axis=-1), vec_mid[0], vec_mid[1], d_wo, vec_mid[2], d_wg, vec_mid[3]), 'dap')
     summed = list(summed)
-    summed[2] = from_group(summed[2])
+    summed[2] = from_group(summed[2].T)
     summed[3] = from_group(summed[3])
     return (d_z,) + tuple(piece.astype(BF16) for piece in summed)
 

time: 806 us -> 756 us (0.938)
  Pallas kernels: 629 us -> 538 us
  waiting for transfers between devices: 107 us -> 149 us
    ppermute x21, waiting for transfers between devices: 107 us -> 149 us  [local_step(): lax.ppermute(arr, 'dap', [(d, d ^ bit) for d in range(n_dap)])]
    pallas_call x5, Pallas kernels: 155 us -> 120 us  [project(): pl.pallas_call(functools.partial(project_kernel, keep_norm), grid=(rows /...]
    pallas_call x2, Pallas kernels: 141 us -> 109 us  [final(): pl.pallas_call(functools.partial(final_kernel, bool(seeds)), grid_spec=pl...]
    pallas_call x4, Pallas kernels: 198 us -> 174 us  [middle(): pl.pallas_call(functools.partial(middle_kernel, n_mul, n_mid, len(b_parts...]
  transfers between devices with their start and end apart: 21 -> 21, of which waited for: 7 -> 8; matrix products, arithmetic and copies ran while one was open for 3% -> 3% of each run, Pallas kernels for 57% -> 54%
where the time goes in v1:
time: 756 us
  Pallas kernels  538 us (71%)
  waiting for transfers between devices  149 us (20%)
  local copies, waits for them, and re-layouts  27.7 us (4%)
  blocking collectives  16.5 us (2%)
  starting transfers between devices  13.1 us (2%)
  other arithmetic  9.94 us (1%)
    pallas_call x4, Pallas kernels, middle(): pl.pallas_call(functools.partial(middle_kernel, n_mul, n_mid, len(b_parts...  174 us
    ppermute x21, waiting for transfers between devices, local_step(): lax.ppermute(arr, 'dap', [(d, d ^ bit) for d in range(n_dap)])  149 us
    pallas_call x5, Pallas kernels, grad_sum(): pl.pallas_call(functools.partial(grad_kernel, trans, len(grads), len(acts...  135 us
    pallas_call x5, Pallas kernels, project(): pl.pallas_call(functools.partial(project_kernel, keep_norm), grid=(rows /...  120 us
    pallas_call x2, Pallas kernels, final(): pl.pallas_call(functools.partial(final_kernel, bool(seeds)), grid_spec=pl...  109 us
    psum x1, blocking collectives, local_step(): lax.psum((vec_in[0], vec_in[1], dw_t, jnp.sum(dbin, axis=-1), vec_mid[0],...  16.5 us
  transfers between devices with their start and end apart: 21, of which 8 were waited for; matrix products, arithmetic and copies ran while one was open for 3% of the time, Pallas kernels for 54%

profile of v1, /device:TPU:0, one launch (start us, length us, event | category | flops | bytes accessed | tf_op | source)
XLA Modules:
  0.0 755.7 jit_solution(4186869738878335285)
XLA Ops:
  0.6 2.0 reshape.48.mask_ref
  6.0 1.4 broadcast_in_dim.19.scale_ref
  7.4 1.4 broadcast_in_dim.20.offset_ref
  8.8 55.3 %project.5 = (bf16[128,128,512]{2,1,0:T(8,128)(2,1)}, bf16[128,128,512]{2,1,0:T(8,128)(2,1)}, bf16[128,512,128]{2,1,0:T(8,128)(2,1)}) custom-call(bf16[128,512,128]{2,1,0:T(8,128)(2,1)} %z_ref.5, s32[128,4,1,128]{3,2,1,0:T(1,128)} %reshape.48.mask_ref, bf16[512,256]{1,0:T(8,128)(2,1)} %maximum_maximum_fusion.w_ref, f32[128,256]{1,0:T(8,128)} %broadcast_in_dim.19.scale_ref, ...), custom_call_target="tpu_custom_call" | custom-call | flops 25600000000 | bytes 67108864 | tf_op jit(solution)/shard_map/project/pallas_call | solution.py:115
  65.0 3.0 collective-permute-start.1
  68.0 4.6 slice.31
  72.7 9.0 %fusion = (bf16[32,512,128]{2,1,0:T(8,128)(2,1)}, bf16[32,512,128]{2,1,0:T(8,128)(2,1)}, bf16[32,512,128]{2,1,0:T(8,128)(2,1)}) fusion(bf16[128,512,128]{2,1,0:T(8,128)(2,1)} %z_ref.5), kind=kLoop, calls=%fused_computation.18 | loop fusion | bytes 25165824 | tf_op jit(solution)/shard_map/slice | solution.py:428
  81.7 2.0 collective-permute-start.4
  87.6 43.6 %middle.4 = (bf16[128,64,128]{2,1,0:T(8,128)(2,1)}, bf16[128,64,128]{2,1,0:T(8,128)(2,1)}, bf16[128,128,128]{2,1,0:T(8,128)(2,1)}, f32[128,128]{1,0:T(8,128)}, f...) custom-call(s32[2]{0:T(128)} %pad_add_fusion.4.idx_ref, bf16[128,128,512]{2,1,0:T(8,128)(2,1)} %get-tuple-element.54.a_ref.refs_4_, ...), custom_call_target="tpu_custom_call" | custom-call | flops 24999999488 | bytes 50331648 | tf_op jit(solution)/shard_map/middle/pallas_call | solution.py:216
  131.2 43.5 %middle.5 = (bf16[128,64,128]{2,1,0:T(8,128)(2,1)}, bf16[128,64,128]{2,1,0:T(8,128)(2,1)}, bf16[128,128,128]{2,1,0:T(8,128)(2,1)}, f32[128,128]{1,0:T(8,128)}, f...) custom-call(s32[2]{0:T(128)} %pad_add_fusion.3.idx_ref, bf16[128,128,512]{2,1,0:T(8,128)(2,1)} %get-tuple-element.54.a_ref.refs_4_, ...), custom_call_target="tpu_custom_call" | custom-call | flops 24999999488 | bytes 50331648 | tf_op jit(solution)/shard_map/middle/pallas_call | solution.py:216
  175.4 16.2 %project.6 = (bf16[128,32,512]{2,1,0:T(8,128)(2,1)}, bf16[128,32,512]{2,1,0:T(8,128)(2,1)}) custom-call(bf16[32,512,128]{2,1,0:T(8,128)(2,1)} %collective-permute-done.2.z_ref, s32[128,4,1,128]{3,2,1,0:T(1,128)} %copy-done.7, bf16[512,256]{1,0:T(8,128)(2,1)} %maximum_maximum_fusion.w_ref, f32[128,256]{1,0:T(8,128)} %broadcast_in_dim.19.scale_ref, ...), custom_call_target="tpu_custom_call" | custom-call | flops 6400000000 | bytes 16777216 | tf_op jit(solution)/shard_map/project/pallas_call | solution.py:115
  191.7 63.4 %collective-permute-done.4.z_ref = bf16[32,512,128]{2,1,0:T(8,128)(2,1)} collective-permute-done((bf16[32,512,128]{2,1,0:T(8,128)(2,1)}, bf16[32,512,128]{2,1,0:T(8,128)(2,1)}, u32[]{:S(2)}, u32[]{:S(2)}) %collective-permute-start.4) | collective-permute-done | bytes 4194336 | tf_op jit(solution)/shard_map/ppermute | solution.py:413
  255.1 16.3 %project.7 = (bf16[128,32,512]{2,1,0:T(8,128)(2,1)}, bf16[128,32,512]{2,1,0:T(8,128)(2,1)}) custom-call(bf16[32,512,128]{2,1,0:T(8,128)(2,1)} %collective-permute-done.4.z_ref, s32[128,4,1,128]{3,2,1,0:T(1,128)} %copy-done.7, bf16[512,256]{1,0:T(8,128)(2,1)} %maximum_maximum_fusion.w_ref, f32[128,256]{1,0:T(8,128)} %broadcast_in_dim.19.scale_ref, ...), custom_call_target="tpu_custom_call" | custom-call | flops 6400000000 | bytes 16777216 | tf_op jit(solution)/shard_map/project/pallas_call | solution.py:115
  273.6 8.3 %collective-permute-done.7.refs_1_ = bf16[128,64,128]{2,1,0:T(8,128)(2,1)} collective-permute-done((bf16[128,64,128]{2,1,0:T(8,128)(2,1)S(1)}, bf16[128,64,128]{2,1,0:T(8,128)(2,1)}, u32[]{:S(2)}, u32[]{:S(2)}) %collective-permute-start.7) | collective-permute-done | bytes 2097184 | tf_op jit(solution)/shard_map/ppermute | solution.py:413
  282.9 2.0 collective-permute-done.8.refs_3_
  285.0 27.5 %shard_map.212.refs_13_.refs_10_ = f32[128,128,512]{2,1,0:T(8,128)} custom-call(bf16[128,64,128]{2,1,0:T(8,128)(2,1)} %get-tuple-element.62.refs_0_, bf16[128,64,128]{2,1,0:T(8,128)(2,1)} %collective-permute-done.7.refs_1_, bf16[128,64,128]{2,1,0:T(8,128)(2,1)} %get-tuple-element.64.refs_2_.refs_1_, bf16[128,64,128]{2,1,0:T(8,128)(2,1)} %collective-permute-done.8.refs_3_, ...), custom_call_target="tpu_custom_call" | custom-call | flops 12000000000 | bytes 83886080 | tf_op jit(solution)/shard_map/pallas_call | solution.py:303
  312.5 43.3 %middle.6 = (bf16[128,64,128]{2,1,0:T(8,128)(2,1)}, bf16[128,64,128]{2,1,0:T(8,128)(2,1)}, bf16[128,128,128]{2,1,0:T(8,128)(2,1)}, f32[128,128]{1,0:T(8,128)}, f...) custom-call(s32[2]{0:T(128)} %pad_add_fusion.2.idx_ref, bf16[128,128,512]{2,1,0:T(8,128)(2,1)} %get-tuple-element.54.a_ref.refs_4_, ...), custom_call_target="tpu_custom_call" | custom-call | flops 24999999488 | bytes 50331648 | tf_op jit(solution)/shard_map/middle/pallas_call | solution.py:216
  355.8 9.9 %collective-permute-done.z_ref = bf16[32,512,128]{2,1,0:T(8,128)(2,1)} collective-permute-done((bf16[32,512,128]{2,1,0:T(8,128)(2,1)}, bf16[32,512,128]{2,1,0:T(8,128)(2,1)}, u32[]{:S(2)}, u32[]{:S(2)}) %collective-permute-start) | collective-permute-done | bytes 4194336 | tf_op jit(solution)/shard_map/ppermute | solution.py:413
  365.7 16.2 %project.8 = (bf16[128,32,512]{2,1,0:T(8,128)(2,1)}, bf16[128,32,512]{2,1,0:T(8,128)(2,1)}) custom-call(bf16[32,512,128]{2,1,0:T(8,128)(2,1)} %collective-permute-done.z_ref, s32[128,4,1,128]{3,2,1,0:T(1,128)} %copy-done.7, bf16[512,256]{1,0:T(8,128)(2,1)} %maximum_maximum_fusion.w_ref, f32[128,256]{1,0:T(8,128)} %broadcast_in_dim.19.scale_ref, ...), custom_call_target="tpu_custom_call" | custom-call | flops 6400000000 | bytes 16777216 | tf_op jit(solution)/shard_map/project/pallas_call | solution.py:115
  381.9 33.8 %shard_map.213.refs_0_.refs_6_ = f32[128,128,512]{2,1,0:T(8,128)} custom-call(bf16[128,64,128]{2,1,0:T(8,128)(2,1)} %get-tuple-element.62.refs_0_, bf16[128,64,128]{2,1,0:T(8,128)(2,1)} %get-tuple-element.64.refs_2_.refs_1_, bf16[128,64,128]{2,1,0:T(8,128)(2,1)} %get-tuple-element.63.refs_2_, bf16[128,64,128]{2,1,0:T(8,128)(2,1)} %get-tuple-element.65.refs_3_, ...), custom_call_target="tpu_custom_call" | custom-call | flops 12000000000 | bytes 83886080 | tf_op jit(solution)/shard_map/pallas_call | solution.py:303
  415.7 39.4 %collective-permute-done.10.z_ref = bf16[32,512,128]{2,1,0:T(8,128)(2,1)} collective-permute-done((bf16[32,512,128]{2,1,0:T(8,128)(2,1)}, bf16[32,512,128]{2,1,0:T(8,128)(2,1)}, u32[]{:S(2)}, u32[]{:S(2)}) %collective-permute-start.10) | collective-permute-done | bytes 4194336 | tf_op jit(solution)/shard_map/ppermute | solution.py:413
  455.1 16.2 %project.9 = (bf16[128,32,512]{2,1,0:T(8,128)(2,1)}, bf16[128,32,512]{2,1,0:T(8,128)(2,1)}) custom-call(bf16[32,512,128]{2,1,0:T(8,128)(2,1)} %collective-permute-done.10.z_ref, s32[128,4,1,128]{3,2,1,0:T(1,128)} %copy-done.7, bf16[512,256]{1,0:T(8,128)(2,1)} %maximum_maximum_fusion.w_ref, f32[128,256]{1,0:T(8,128)} %broadcast_in_dim.19.scale_ref, ...), custom_call_target="tpu_custom_call" | custom-call | flops 6400000000 | bytes 16777216 | tf_op jit(solution)/shard_map/project/pallas_call | solution.py:115
  476.2 2.6 collective-permute-done.12.refs_3_.refs_5_
  479.6 43.3 %middle.7 = (bf16[128,64,128]{2,1,0:T(8,128)(2,1)}, bf16[128,64,128]{2,1,0:T(8,128)(2,1)}, bf16[128,128,128]{2,1,0:T(8,128)(2,1)}, f32[128,128]{1,0:T(8,128)}, f...) custom-call(s32[2]{0:T(128)} %pad_add_fusion.1.idx_ref, bf16[128,128,512]{2,1,0:T(8,128)(2,1)} %get-tuple-element.54.a_ref.refs_4_, ...), custom_call_target="tpu_custom_call" | custom-call | flops 24999999488 | bytes 50331648 | tf_op jit(solution)/shard_map/middle/pallas_call | solution.py:216
  525.0 27.0 %shard_map.214.refs_12_.da_ref = bf16[128,128,512]{2,1,0:T(8,128)(2,1)} custom-call(bf16[128,64,128]{2,1,0:T(8,128)(2,1)} %get-tuple-element.74.refs_0_, bf16[128,64,128]{2,1,0:T(8,128)(2,1)} %get-tuple-element.75.refs_1_, bf16[128,32,512]{2,1,0:T(8,128)(2,1)} %get-tuple-element.68.refs_0_.refs_2_, bf16[128,32,512]{2,1,0:T(8,128)(2,1)} %get-tuple-element.72.refs_1_.refs_3_, ...), custom_call_target="tpu_custom_call" | custom-call | flops 12000000000 | bytes 83886080 | tf_op jit(solution)/shard_map/pallas_call | solution.py:303
  553.7 13.6 %collective-permute-done.20.refs_1_ = bf16[128,64,128]{2,1,0:T(8,128)(2,1)} collective-permute-done((bf16[128,64,128]{2,1,0:T(8,128)(2,1)S(1)}, bf16[128,64,128]{2,1,0:T(8,128)(2,1)}, u32[]{:S(2)}, u32[]{:S(2)}) %collective-permute-start.20) | collective-permute-done | bytes 2097184 | tf_op jit(solution)/shard_map/ppermute | solution.py:413
  567.3 23.3 %shard_map.215.db_ref = bf16[64,128,512]{2,1,0:T(8,128)(2,1)} custom-call(bf16[128,64,128]{2,1,0:T(8,128)(2,1)} %collective-permute-done.19.refs_0_, bf16[128,64,128]{2,1,0:T(8,128)(2,1)} %collective-permute-done.20.refs_1_, bf16[128,32,512]{2,1,0:T(8,128)(2,1)} %get-tuple-element.60.refs_0_.refs_2_, ...), custom_call_target="tpu_custom_call" | custom-call | flops 12000000000 | bytes 83886080 | tf_op jit(solution)/shard_map/pallas_call | solution.py:303
  592.2 54.5 %final.2 = (bf16[128,512,128]{2,1,0:T(8,128)(2,1)}, f32[512,128]{1,0:T(8,128)}, f32[512,128]{1,0:T(8,128)}, f32[2,128,128]{2,1,0:T(8,128)}) custom-call(s32[4]{0:T(128)} %pad_add_fusion.q_ref, bf16[128,512,128]{2,1,0:T(8,128)(2,1)} %z_ref.5, bf16[128,512,128]{2,1,0:T(8,128)(2,1)} %dy_ref.3, bf16[128,128,512]{2,1,0:T(8,128)(2,1)} %shard_map.214.refs_12_.da_ref, ...), custom_call_target="tpu_custom_call" | custom-call | flops 30000001024 | bytes 67108864 | tf_op jit(solution)/shard_map/final/pallas_call | solution.py:390
  646.7 10.2 %collective-permute-done.14.refs_1_ = bf16[128,64,128]{2,1,0:T(8,128)(2,1)} collective-permute-done((bf16[128,64,128]{2,1,0:T(8,128)(2,1)}, bf16[128,64,128]{2,1,0:T(8,128)(2,1)}, u32[]{:S(2)}, u32[]{:S(2)}) %collective-permute-start.14) | collective-permute-done | bytes 2097184 | tf_op jit(solution)/shard_map/ppermute | solution.py:413
  656.8 23.3 %shard_map.216.db_ref = bf16[64,128,512]{2,1,0:T(8,128)(2,1)} custom-call(bf16[128,64,128]{2,1,0:T(8,128)(2,1)} %collective-permute-done.13.refs_0_, bf16[128,64,128]{2,1,0:T(8,128)(2,1)} %collective-permute-done.14.refs_1_, bf16[128,32,512]{2,1,0:T(8,128)(2,1)} %get-tuple-element.60.refs_0_.refs_2_, ...), custom_call_target="tpu_custom_call" | custom-call | flops 12000000000 | bytes 83886080 | tf_op jit(solution)/shard_map/pallas_call | solution.py:303
  680.1 54.7 %final.3 = (bf16[128,512,128]{2,1,0:T(8,128)(2,1)}, f32[512,128]{1,0:T(8,128)}, f32[512,128]{1,0:T(8,128)}, f32[2,128,128]{2,1,0:T(8,128)}) custom-call(s32[4]{0:T(128)} %pad_add_fusion.q_ref, bf16[128,512,128]{2,1,0:T(8,128)(2,1)} %z_ref.5, bf16[128,512,128]{2,1,0:T(8,128)(2,1)} %dy_ref.3, ...), custom_call_target="tpu_custom_call", output_to_operand_aliasing={{0}: (16, {})} | custom-call | flops 30000001024 | bytes 67108864 | tf_op jit(solution)/shard_map/final/pallas_call | solution.py:390
  736.9 16.5 %all-reduce.2 = (bf16[128]{0:T(256)(128)(2,1)}, bf16[128]{0:T(256)(128)(2,1)}, bf16[512,128]{1,0:T(8,128)(2,1)S(1)}, bf16[512]{0:T(512)(128)(2,1)S(1)}, bf16[128...) all-reduce(f32[128]{0:T(128)S(1)} %get-tuple-element.148, ...), channel_id=1, replica_groups=mesh['batch'=2,'dap'=4] {'dap'}, use_global_device_ids=true, to_apply=%region_1.0 | all-reduce | flops 99584 | bytes 597504 | tf_op jit(solution)/shard_map/psum | solution.py:472
  (119 shorter events, 27.5 us)
Async XLA Ops:
  8.8 56.2 %copy-start.8 = (s32[128,4,1,128]{3,2,1,0:T(1,128)S(1)}, s32[128,4,1,128]{3,2,1,0:T(1,128)}, u32[]{:S(2)}) copy-start(s32[128,4,1,128]{3,2,1,0:T(1,128)} %reshape.48.mask_ref) | copy-start | bytes 786436
  64.2 67.0 %collective-permute-start.3 = (bf16[128,128,512]{2,1,0:T(8,128)(2,1)}, bf16[128,128,512]{2,1,0:T(8,128)(2,1)}, u32[]{:S(2)}, u32[]{:S(2)}) collective-permute-start(bf16[128,128,512]{2,1,0:T(8,128)(2,1)} %get-tuple-element.55.refs_0_.refs_6_), channel_id=1, source_target_pairs={{0,1},{1,0},{2,3},{3,2},{4,5},{5,4},{6,7},{7,6}} | collective-permute-start | bytes 50331656 | tf_op jit(solution)/shard_map/ppermute | solution.py:413
  65.0 206.9 %collective-permute-start.9 = (bf16[128,128,512]{2,1,0:T(8,128)(2,1)}, bf16[128,128,512]{2,1,0:T(8,128)(2,1)}, u32[]{:S(2)}, u32[]{:S(2)}) collective-permute-start(bf16[128,128,512]{2,1,0:T(8,128)(2,1)} %get-tuple-element.54.a_ref.refs_4_), channel_id=1, source_target_pairs={{0,1},{1,0},{2,3},{3,2},{4,5},{5,4},{6,7},{7,6}} | collective-permute-start | bytes 50331656 | tf_op jit(solution)/shard_map/ppermute | solution.py:413
  65.0 109.7 %collective-permute-start.1 = (s32[128,4,1,128]{3,2,1,0:T(1,128)S(1)}, s32[128,4,1,128]{3,2,1,0:T(1,128)S(1)}, u32[]{:S(2)}, u32[]{:S(2)}) collective-permute-start(s32[128,4,1,128]{3,2,1,0:T(1,128)S(1)} %copy-done.8), channel_id=1, source_target_pairs={{0,2},{1,3},{2,0},{3,1},{4,6},{5,7},{6,4},{7,5}} | collective-permute-start | bytes 786440 | tf_op jit(solution)/shard_map/ppermute | solution.py:413
  72.6 102.1 %collective-permute-start.2 = (bf16[32,512,128]{2,1,0:T(8,128)(2,1)}, bf16[32,512,128]{2,1,0:T(8,128)(2,1)}, u32[]{:S(2)}, u32[]{:S(2)}) collective-permute-start(bf16[32,512,128]{2,1,0:T(8,128)(2,1)} %slice.31), channel_id=1, source_target_pairs={{0,2},{1,3},{2,0},{3,1},{4,6},{5,7},{6,4},{7,5}} | collective-permute-start | bytes 12582920 | tf_op jit(solution)/shard_map/ppermute | solution.py:413
  81.7 173.4 %collective-permute-start.4 = (bf16[32,512,128]{2,1,0:T(8,128)(2,1)}, bf16[32,512,128]{2,1,0:T(8,128)(2,1)}, u32[]{:S(2)}, u32[]{:S(2)}) collective-permute-start(bf16[32,512,128]{2,1,0:T(8,128)(2,1)} %get-tuple-element.141), channel_id=1, source_target_pairs={{0,2},{1,3},{2,0},{3,1},{4,6},{5,7},{6,4},{7,5}} | collective-permute-start | bytes 12582920 | tf_op jit(solution)/shard_map/ppermute | solution.py:413
  191.7 120.8 %collective-permute-start.5 = (bf16[128,32,512]{2,1,0:T(8,128)(2,1)}, bf16[128,32,512]{2,1,0:T(8,128)(2,1)}, u32[]{:S(2)}, u32[]{:S(2)}) collective-permute-start(bf16[128,32,512]{2,1,0:T(8,128)(2,1)} %get-tuple-element.59.refs_0_.refs_8_), channel_id=1, source_target_pairs={{0,1},{1,0},{2,3},{3,2},{4,5},{5,4},{6,7},{7,6}} | collective-permute-start | bytes 12582920 | tf_op jit(solution)/shard_map/ppermute | solution.py:413
  271.4 41.1 %collective-permute-start.6 = (bf16[128,32,512]{2,1,0:T(8,128)(2,1)}, bf16[128,32,512]{2,1,0:T(8,128)(2,1)}, u32[]{:S(2)}, u32[]{:S(2)}) collective-permute-start(bf16[128,32,512]{2,1,0:T(8,128)(2,1)} %get-tuple-element.61.refs_1_.refs_9_), channel_id=1, source_target_pairs={{0,1},{1,0},{2,3},{3,2},{4,5},{5,4},{6,7},{7,6}} | collective-permute-start | bytes 12582920 | tf_op jit(solution)/shard_map/ppermute | solution.py:413
  271.4 10.5 %collective-permute-start.7 = (bf16[128,64,128]{2,1,0:T(8,128)(2,1)S(1)}, bf16[128,64,128]{2,1,0:T(8,128)(2,1)}, u32[]{:S(2)}, u32[]{:S(2)}) collective-permute-start(bf16[128,64,128]{2,1,0:T(8,128)(2,1)S(1)} %copy-done.1), channel_id=1, source_target_pairs={{0,1},{1,0},{2,3},{3,2},{4,5},{5,4},{6,7},{7,6}} | collective-permute-start | bytes 6291464 | tf_op jit(solution)/shard_map/ppermute | solution.py:413
  271.9 13.0 %collective-permute-start.8 = (bf16[128,64,128]{2,1,0:T(8,128)(2,1)}, bf16[128,64,128]{2,1,0:T(8,128)(2,1)}, u32[]{:S(2)}, u32[]{:S(2)}) collective-permute-start(bf16[128,64,128]{2,1,0:T(8,128)(2,1)} %get-tuple-element.65.refs_3_), channel_id=1, source_target_pairs={{0,1},{1,0},{2,3},{3,2},{4,5},{5,4},{6,7},{7,6}} | collective-permute-start | bytes 6291464 | tf_op jit(solution)/shard_map/ppermute | solution.py:413
  271.9 93.8 %collective-permute-start = (bf16[32,512,128]{2,1,0:T(8,128)(2,1)}, bf16[32,512,128]{2,1,0:T(8,128)(2,1)}, u32[]{:S(2)}, u32[]{:S(2)}) collective-permute-start(bf16[32,512,128]{2,1,0:T(8,128)(2,1)} %get-tuple-element.142), channel_id=1, source_target_pairs={{0,2},{1,3},{2,0},{3,1},{4,6},{5,7},{6,4},{7,5}} | collective-permute-start | bytes 12582920 | tf_op jit(solution)/shard_map/ppermute | solution.py:413
  281.9 173.2 %collective-permute-start.10 = (bf16[32,512,128]{2,1,0:T(8,128)(2,1)}, bf16[32,512,128]{2,1,0:T(8,128)(2,1)}, u32[]{:S(2)}, u32[]{:S(2)}) collective-permute-start(bf16[32,512,128]{2,1,0:T(8,128)(2,1)} %get-tuple-element.140), channel_id=1, source_target_pairs={{0,2},{1,3},{2,0},{3,1},{4,6},{5,7},{6,4},{7,5}} | collective-permute-start | bytes 12582920 | tf_op jit(solution)/shard_map/ppermute | solution.py:413
  284.9 189.0 %collective-permute-start.15 = (bf16[128,32,512]{2,1,0:T(8,128)(2,1)}, bf16[128,32,512]{2,1,0:T(8,128)(2,1)}, u32[]{:S(2)}, u32[]{:S(2)}) collective-permute-start(bf16[128,32,512]{2,1,0:T(8,128)(2,1)} %get-tuple-element.60.refs_0_.refs_2_), channel_id=1, source_target_pairs={{0,1},{1,0},{2,3},{3,2},{4,5},{5,4},{6,7},{7,6}} | collective-permute-start | bytes 12582920 | tf_op jit(solution)/shard_map/ppermute | solution.py:413
  381.9 93.2 %collective-permute-start.11 = (bf16[128,32,512]{2,1,0:T(8,128)(2,1)}, bf16[128,32,512]{2,1,0:T(8,128)(2,1)}, u32[]{:S(2)}, u32[]{:S(2)}) collective-permute-start(bf16[128,32,512]{2,1,0:T(8,128)(2,1)} %get-tuple-element.68.refs_0_.refs_2_), channel_id=1, source_target_pairs={{0,1},{1,0},{2,3},{3,2},{4,5},{5,4},{6,7},{7,6}} | collective-permute-start | bytes 12582920 | tf_op jit(solution)/shard_map/ppermute | solution.py:413
  415.6 55.6 %copy-start.5 = (s32[128,512]{1,0:T(8,128)S(1)}, s32[128,512]{1,0:T(8,128)}, u32[]{:S(2)}) copy-start(s32[128,512]{1,0:T(8,128)} %param.14) | copy-start | bytes 786436
  415.7 56.4 %copy-start.3 = (bf16[128,8,4,16]{0,3,2,1:T(8,128)(2,1)S(1)}, bf16[128,8,4,16]{0,3,2,1:T(8,128)(2,1)}, u32[]{:S(2)}) copy-start(bf16[128,8,4,16]{0,3,2,1:T(8,128)(2,1)} %copy-done.2) | copy-start | bytes 393220
  415.7 57.1 %copy-start.12 = (bf16[128,128]{1,0:T(8,128)(2,1)S(1)}, bf16[128,128]{1,0:T(8,128)(2,1)}, u32[]{:S(2)}) copy-start(bf16[128,128]{1,0:T(8,128)(2,1)} %param.24) | copy-start | bytes 98308
  415.7 63.1 %copy-start = (bf16[128,64,128]{2,1,0:T(8,128)(2,1)S(1)}, bf16[128,64,128]{2,1,0:T(8,128)(2,1)}, u32[]{:S(2)}) copy-start(bf16[128,64,128]{2,1,0:T(8,128)(2,1)} %get-tuple-element.70.refs_5_) | copy-start | bytes 6291460
  471.3 7.5 collective-permute-start.12
  473.4 78.5 %collective-permute-start.16 = (bf16[128,32,512]{2,1,0:T(8,128)(2,1)}, bf16[128,32,512]{2,1,0:T(8,128)(2,1)}, u32[]{:S(2)}, u32[]{:S(2)}) collective-permute-start(bf16[128,32,512]{2,1,0:T(8,128)(2,1)} %get-tuple-element.66.refs_6_.refs_3_), channel_id=1, source_target_pairs={{0,1},{1,0},{2,3},{3,2},{4,5},{5,4},{6,7},{7,6}} | collective-permute-start | bytes 12582920 | tf_op jit(solution)/shard_map/ppermute | solution.py:413
  473.9 93.4 %collective-permute-start.17 = (bf16[128,32,512]{2,1,0:T(8,128)(2,1)}, bf16[128,32,512]{2,1,0:T(8,128)(2,1)}, u32[]{:S(2)}, u32[]{:S(2)}) collective-permute-start(bf16[128,32,512]{2,1,0:T(8,128)(2,1)} %get-tuple-element.71.refs_12_.refs_4_), channel_id=1, source_target_pairs={{0,1},{1,0},{2,3},{3,2},{4,5},{5,4},{6,7},{7,6}} | collective-permute-start | bytes 12582920 | tf_op jit(solution)/shard_map/ppermute | solution.py:413
  473.9 93.4 %collective-permute-start.18 = (bf16[128,32,512]{2,1,0:T(8,128)(2,1)}, bf16[128,32,512]{2,1,0:T(8,128)(2,1)}, u32[]{:S(2)}, u32[]{:S(2)}) collective-permute-start(bf16[128,32,512]{2,1,0:T(8,128)(2,1)} %get-tuple-element.73.refs_13_.refs_5_), channel_id=1, source_target_pairs={{0,1},{1,0},{2,3},{3,2},{4,5},{5,4},{6,7},{7,6}} | collective-permute-start | bytes 12582920 | tf_op jit(solution)/shard_map/ppermute | solution.py:413
  475.0 49.0 %copy-start.13 = (f32[128,128]{1,0:T(8,128)S(1)}, f32[128,128]{1,0:T(8,128)}, u32[]{:S(2)}) copy-start(f32[128,128]{1,0:T(8,128)} %get-tuple-element.89) | copy-start | bytes 196612
  475.0 49.0 %copy-start.14 = (f32[128,128]{1,0:T(8,128)S(1)}, f32[128,128]{1,0:T(8,128)}, u32[]{:S(2)}) copy-start(f32[128,128]{1,0:T(8,128)} %get-tuple-element.93) | copy-start | bytes 196612
  475.1 49.0 %copy-start.15 = (f32[128,128]{1,0:T(8,128)S(1)}, f32[128,128]{1,0:T(8,128)}, u32[]{:S(2)}) copy-start(f32[128,128]{1,0:T(8,128)} %get-tuple-element.90) | copy-start | bytes 196612
  475.1 49.0 %copy-start.16 = (f32[128,128]{1,0:T(8,128)S(1)}, f32[128,128]{1,0:T(8,128)}, u32[]{:S(2)}) copy-start(f32[128,128]{1,0:T(8,128)} %get-tuple-element.94) | copy-start | bytes 196612
  475.1 49.0 %copy-start.17 = (f32[128,128]{1,0:T(8,128)S(1)}, f32[128,128]{1,0:T(8,128)}, u32[]{:S(2)}) copy-start(f32[128,128]{1,0:T(8,128)} %get-tuple-element.91) | copy-start | bytes 196612
  475.1 49.0 %copy-start.18 = (f32[128,128]{1,0:T(8,128)S(1)}, f32[128,128]{1,0:T(8,128)}, u32[]{:S(2)}) copy-start(f32[128,128]{1,0:T(8,128)} %get-tuple-element.95) | copy-start | bytes 196612
  475.1 77.9 %collective-permute-start.19 = (bf16[128,64,128]{2,1,0:T(8,128)(2,1)}, bf16[128,64,128]{2,1,0:T(8,128)(2,1)}, u32[]{:S(2)}, u32[]{:S(2)}) collective-permute-start(bf16[128,64,128]{2,1,0:T(8,128)(2,1)} %get-tuple-element.69.refs_4_), channel_id=1, source_target_pairs={{0,2},{1,3},{2,0},{3,1},{4,6},{5,7},{6,4},{7,5}} | collective-permute-start | bytes 6291464 | tf_op jit(solution)/shard_map/ppermute | solution.py:413
  478.8 88.5 %collective-permute-start.20 = (bf16[128,64,128]{2,1,0:T(8,128)(2,1)S(1)}, bf16[128,64,128]{2,1,0:T(8,128)(2,1)}, u32[]{:S(2)}, u32[]{:S(2)}) collective-permute-start(bf16[128,64,128]{2,1,0:T(8,128)(2,1)S(1)} %copy-done), channel_id=1, source_target_pairs={{0,3},{1,2},{2,1},{3,0},{4,7},{5,6},{6,5},{7,4}} | collective-permute-start | bytes 6291464 | tf_op jit(solution)/shard_map/ppermute | solution.py:413
  552.0 94.7 %collective-permute-start.13 = (bf16[128,64,128]{2,1,0:T(8,128)(2,1)}, bf16[128,64,128]{2,1,0:T(8,128)(2,1)}, u32[]{:S(2)}, u32[]{:S(2)}) collective-permute-start(bf16[128,64,128]{2,1,0:T(8,128)(2,1)} %get-tuple-element.74.refs_0_), channel_id=1, source_target_pairs={{0,2},{1,3},{2,0},{3,1},{4,6},{5,7},{6,4},{7,5}} | collective-permute-start | bytes 6291464 | tf_op jit(solution)/shard_map/ppermute | solution.py:413
  553.0 103.8 %collective-permute-start.14 = (bf16[128,64,128]{2,1,0:T(8,128)(2,1)}, bf16[128,64,128]{2,1,0:T(8,128)(2,1)}, u32[]{:S(2)}, u32[]{:S(2)}) collective-permute-start(bf16[128,64,128]{2,1,0:T(8,128)(2,1)} %get-tuple-element.75.refs_1_), channel_id=1, source_target_pairs={{0,3},{1,2},{2,1},{3,0},{4,7},{5,6},{6,5},{7,4}} | collective-permute-start | bytes 6291464 | tf_op jit(solution)/shard_map/ppermute | solution.py:413
  (14 other events, 312.2 us)

commit v2 on v1

--- a/solution.py
+++ b/solution.py
@@ -86,7 +86,7 @@
                         scr[pl.ds(at, GROUP, stride=pitch), :] = val[:, t * LANES:(t + 1) * LANES]
         return carry
 
-    lax.fori_loop(0, ROWS, row, 0, unroll=2)
+    lax.fori_loop(0, ROWS, row, 0, unroll=4)
 
     def pack(c, carry):
         for t in range(n_lane):
@@ -188,7 +188,7 @@
             dwg_ref[...] += dot_nn(gate16, zn)
             return carry
 
-        lax.fori_loop(0, MID_ROWS // 2, pair, 0, unroll=2)
+        lax.fori_loop(0, MID_ROWS // 2, pair, 0, unroll=4)
 
     @pl.when(step >= n_mul + n_mid)
     def _():
@@ -366,7 +366,7 @@
             dz_ref[i, pl.ds(offs[t], LANES), :] = out.astype(BF16)
         return carry
 
-    lax.fori_loop(0, ROWS, row, 0, unroll=2)
+    lax.fori_loop(0, ROWS, row, 0, unroll=4)
 
 
 def final(q_all, z_rows, dy_rows, d_a, d_b, gates, w_t, w_back, scale, offset, first, d_z=None, seeds=()):

time: 756 us -> 733 us (0.970)
  Pallas kernels: 538 us -> 490 us
  waiting for transfers between devices: 149 us -> 174 us
    ppermute x21, waiting for transfers between devices: 149 us -> 174 us  [local_step(): lax.ppermute(arr, 'dap', [(d, d ^ bit) for d in range(n_dap)])]
    pallas_call x5, Pallas kernels: 120 us -> 97.4 us  [project(): pl.pallas_call(functools.partial(project_kernel, keep_norm), grid=(rows /...]
    pallas_call x2, Pallas kernels: 109 us -> 96.6 us  [final(): pl.pallas_call(functools.partial(final_kernel, bool(seeds)), grid_spec=pl...]
    pallas_call x4, Pallas kernels: 174 us -> 161 us  [middle(): pl.pallas_call(functools.partial(middle_kernel, n_mul, n_mid, len(b_parts...]
  transfers between devices with their start and end apart: 21 -> 21, of which waited for: 8 -> 8; matrix products, arithmetic and copies ran while one was open for 3% -> 3% of each run, Pallas kernels for 54% -> 51%
where the time goes in v2:
time: 733 us; the launch traced here: 732 us
  Pallas kernels  490 us (67%)
  waiting for transfers between devices  174 us (24%)
  local copies, waits for them, and re-layouts  27.7 us (4%)
  blocking collectives  16.5 us (2%)
  starting transfers between devices  13.1 us (2%)
  other arithmetic  9.94 us (1%)
    ppermute x21, waiting for transfers between devices, local_step(): lax.ppermute(arr, 'dap', [(d, d ^ bit) for d in range(n_dap)])  174 us
    pallas_call x4, Pallas kernels, middle(): pl.pallas_call(functools.partial(middle_kernel, n_mul, n_mid, len(b_parts...  161 us
    pallas_call x5, Pallas kernels, grad_sum(): pl.pallas_call(functools.partial(grad_kernel, trans, len(grads), len(acts...  135 us
    pallas_call x5, Pallas kernels, project(): pl.pallas_call(functools.partial(project_kernel, keep_norm), grid=(rows /...  97.4 us
    pallas_call x2, Pallas kernels, final(): pl.pallas_call(functools.partial(final_kernel, bool(seeds)), grid_spec=pl...  96.6 us
    psum x1, blocking collectives, local_step(): lax.psum((vec_in[0], vec_in[1], dw_t, jnp.sum(dbin, axis=-1), vec_mid[0],...  16.5 us
  transfers between devices with their start and end apart: 21, of which 8 were waited for; matrix products, arithmetic and copies ran while one was open for 3% of the time, Pallas kernels for 51%

profile of v2, /device:TPU:0, one launch (start us, length us, event | category | flops | bytes accessed | tf_op | source)
XLA Modules:
  0.0 732.3 jit_solution(13200499047568734635)
XLA Ops:
  0.6 2.0 reshape.48.mask_ref
  6.0 1.4 broadcast_in_dim.19.scale_ref
  7.4 1.4 broadcast_in_dim.20.offset_ref
  8.8 44.0 %project.5 = (bf16[128,128,512]{2,1,0:T(8,128)(2,1)}, bf16[128,128,512]{2,1,0:T(8,128)(2,1)}, bf16[128,512,128]{2,1,0:T(8,128)(2,1)}) custom-call(bf16[128,512,128]{2,1,0:T(8,128)(2,1)} %z_ref.5, s32[128,4,1,128]{3,2,1,0:T(1,128)} %reshape.48.mask_ref, bf16[512,256]{1,0:T(8,128)(2,1)} %maximum_maximum_fusion.w_ref, f32[128,256]{1,0:T(8,128)} %broadcast_in_dim.19.scale_ref, ...), custom_call_target="tpu_custom_call" | custom-call | flops 25600000000 | bytes 67108864 | tf_op jit(solution)/shard_map/project/pallas_call | solution.py:115
  53.6 3.0 collective-permute-start.1
  56.6 4.6 slice.31
  61.3 9.0 %fusion = (bf16[32,512,128]{2,1,0:T(8,128)(2,1)}, bf16[32,512,128]{2,1,0:T(8,128)(2,1)}, bf16[32,512,128]{2,1,0:T(8,128)(2,1)}) fusion(bf16[128,512,128]{2,1,0:T(8,128)(2,1)} %z_ref.5), kind=kLoop, calls=%fused_computation.18 | loop fusion | bytes 25165824 | tf_op jit(solution)/shard_map/slice | solution.py:428
  70.3 2.0 collective-permute-start.4
  76.2 40.5 %middle.4 = (bf16[128,64,128]{2,1,0:T(8,128)(2,1)}, bf16[128,64,128]{2,1,0:T(8,128)(2,1)}, bf16[128,128,128]{2,1,0:T(8,128)(2,1)}, f32[128,128]{1,0:T(8,128)}, f...) custom-call(s32[2]{0:T(128)} %pad_add_fusion.4.idx_ref, bf16[128,128,512]{2,1,0:T(8,128)(2,1)} %get-tuple-element.54.a_ref.refs_4_, ...), custom_call_target="tpu_custom_call" | custom-call | flops 24999999488 | bytes 50331648 | tf_op jit(solution)/shard_map/middle/pallas_call | solution.py:216
  116.8 40.5 %middle.5 = (bf16[128,64,128]{2,1,0:T(8,128)(2,1)}, bf16[128,64,128]{2,1,0:T(8,128)(2,1)}, bf16[128,128,128]{2,1,0:T(8,128)(2,1)}, f32[128,128]{1,0:T(8,128)}, f...) custom-call(s32[2]{0:T(128)} %pad_add_fusion.3.idx_ref, bf16[128,128,512]{2,1,0:T(8,128)(2,1)} %get-tuple-element.54.a_ref.refs_4_, ...), custom_call_target="tpu_custom_call" | custom-call | flops 24999999488 | bytes 50331648 | tf_op jit(solution)/shard_map/middle/pallas_call | solution.py:216
  158.0 13.4 %project.6 = (bf16[128,32,512]{2,1,0:T(8,128)(2,1)}, bf16[128,32,512]{2,1,0:T(8,128)(2,1)}) custom-call(bf16[32,512,128]{2,1,0:T(8,128)(2,1)} %collective-permute-done.2.z_ref, s32[128,4,1,128]{3,2,1,0:T(1,128)} %copy-done.7, bf16[512,256]{1,0:T(8,128)(2,1)} %maximum_maximum_fusion.w_ref, f32[128,256]{1,0:T(8,128)} %broadcast_in_dim.19.scale_ref, ...), custom_call_target="tpu_custom_call" | custom-call | flops 6400000000 | bytes 16777216 | tf_op jit(solution)/shard_map/project/pallas_call | solution.py:115
  171.4 72.3 %collective-permute-done.4.z_ref = bf16[32,512,128]{2,1,0:T(8,128)(2,1)} collective-permute-done((bf16[32,512,128]{2,1,0:T(8,128)(2,1)}, bf16[32,512,128]{2,1,0:T(8,128)(2,1)}, u32[]{:S(2)}, u32[]{:S(2)}) %collective-permute-start.4) | collective-permute-done | bytes 4194336 | tf_op jit(solution)/shard_map/ppermute | solution.py:413
  243.7 13.5 %project.7 = (bf16[128,32,512]{2,1,0:T(8,128)(2,1)}, bf16[128,32,512]{2,1,0:T(8,128)(2,1)}) custom-call(bf16[32,512,128]{2,1,0:T(8,128)(2,1)} %collective-permute-done.4.z_ref, s32[128,4,1,128]{3,2,1,0:T(1,128)} %copy-done.7, bf16[512,256]{1,0:T(8,128)(2,1)} %maximum_maximum_fusion.w_ref, f32[128,256]{1,0:T(8,128)} %broadcast_in_dim.19.scale_ref, ...), custom_call_target="tpu_custom_call" | custom-call | flops 6400000000 | bytes 16777216 | tf_op jit(solution)/shard_map/project/pallas_call | solution.py:115
  259.3 8.3 %collective-permute-done.7.refs_1_ = bf16[128,64,128]{2,1,0:T(8,128)(2,1)} collective-permute-done((bf16[128,64,128]{2,1,0:T(8,128)(2,1)S(1)}, bf16[128,64,128]{2,1,0:T(8,128)(2,1)}, u32[]{:S(2)}, u32[]{:S(2)}) %collective-permute-start.7) | collective-permute-done | bytes 2097184 | tf_op jit(solution)/shard_map/ppermute | solution.py:413
  268.7 2.0 collective-permute-done.8.refs_3_
  270.8 27.5 %shard_map.212.refs_13_.refs_10_ = f32[128,128,512]{2,1,0:T(8,128)} custom-call(bf16[128,64,128]{2,1,0:T(8,128)(2,1)} %get-tuple-element.62.refs_0_, bf16[128,64,128]{2,1,0:T(8,128)(2,1)} %collective-permute-done.7.refs_1_, bf16[128,64,128]{2,1,0:T(8,128)(2,1)} %get-tuple-element.64.refs_2_.refs_1_, bf16[128,64,128]{2,1,0:T(8,128)(2,1)} %collective-permute-done.8.refs_3_, ...), custom_call_target="tpu_custom_call" | custom-call | flops 12000000000 | bytes 83886080 | tf_op jit(solution)/shard_map/pallas_call | solution.py:303
  298.3 40.2 %middle.6 = (bf16[128,64,128]{2,1,0:T(8,128)(2,1)}, bf16[128,64,128]{2,1,0:T(8,128)(2,1)}, bf16[128,128,128]{2,1,0:T(8,128)(2,1)}, f32[128,128]{1,0:T(8,128)}, f...) custom-call(s32[2]{0:T(128)} %pad_add_fusion.2.idx_ref, bf16[128,128,512]{2,1,0:T(8,128)(2,1)} %get-tuple-element.54.a_ref.refs_4_, ...), custom_call_target="tpu_custom_call" | custom-call | flops 24999999488 | bytes 50331648 | tf_op jit(solution)/shard_map/middle/pallas_call | solution.py:216
  338.5 12.9 %collective-permute-done.z_ref = bf16[32,512,128]{2,1,0:T(8,128)(2,1)} collective-permute-done((bf16[32,512,128]{2,1,0:T(8,128)(2,1)}, bf16[32,512,128]{2,1,0:T(8,128)(2,1)}, u32[]{:S(2)}, u32[]{:S(2)}) %collective-permute-start) | collective-permute-done | bytes 4194336 | tf_op jit(solution)/shard_map/ppermute | solution.py:413
  351.4 13.3 %project.8 = (bf16[128,32,512]{2,1,0:T(8,128)(2,1)}, bf16[128,32,512]{2,1,0:T(8,128)(2,1)}) custom-call(bf16[32,512,128]{2,1,0:T(8,128)(2,1)} %collective-permute-done.z_ref, s32[128,4,1,128]{3,2,1,0:T(1,128)} %copy-done.7, bf16[512,256]{1,0:T(8,128)(2,1)} %maximum_maximum_fusion.w_ref, f32[128,256]{1,0:T(8,128)} %broadcast_in_dim.19.scale_ref, ...), custom_call_target="tpu_custom_call" | custom-call | flops 6400000000 | bytes 16777216 | tf_op jit(solution)/shard_map/project/pallas_call | solution.py:115
  364.8 33.7 %shard_map.213.refs_0_.refs_6_ = f32[128,128,512]{2,1,0:T(8,128)} custom-call(bf16[128,64,128]{2,1,0:T(8,128)(2,1)} %get-tuple-element.62.refs_0_, bf16[128,64,128]{2,1,0:T(8,128)(2,1)} %get-tuple-element.64.refs_2_.refs_1_, bf16[128,64,128]{2,1,0:T(8,128)(2,1)} %get-tuple-element.63.refs_2_, bf16[128,64,128]{2,1,0:T(8,128)(2,1)} %get-tuple-element.65.refs_3_, ...), custom_call_target="tpu_custom_call" | custom-call | flops 12000000000 | bytes 83886080 | tf_op jit(solution)/shard_map/pallas_call | solution.py:303
  398.5 42.3 %collective-permute-done.10.z_ref = bf16[32,512,128]{2,1,0:T(8,128)(2,1)} collective-permute-done((bf16[32,512,128]{2,1,0:T(8,128)(2,1)}, bf16[32,512,128]{2,1,0:T(8,128)(2,1)}, u32[]{:S(2)}, u32[]{:S(2)}) %collective-permute-start.10) | collective-permute-done | bytes 4194336 | tf_op jit(solution)/shard_map/ppermute | solution.py:413
  440.8 13.3 %project.9 = (bf16[128,32,512]{2,1,0:T(8,128)(2,1)}, bf16[128,32,512]{2,1,0:T(8,128)(2,1)}) custom-call(bf16[32,512,128]{2,1,0:T(8,128)(2,1)} %collective-permute-done.10.z_ref, s32[128,4,1,128]{3,2,1,0:T(1,128)} %copy-done.7, bf16[512,256]{1,0:T(8,128)(2,1)} %maximum_maximum_fusion.w_ref, f32[128,256]{1,0:T(8,128)} %broadcast_in_dim.19.scale_ref, ...), custom_call_target="tpu_custom_call" | custom-call | flops 6400000000 | bytes 16777216 | tf_op jit(solution)/shard_map/project/pallas_call | solution.py:115
  459.0 2.6 collective-permute-done.12.refs_3_.refs_5_
  462.4 40.1 %middle.7 = (bf16[128,64,128]{2,1,0:T(8,128)(2,1)}, bf16[128,64,128]{2,1,0:T(8,128)(2,1)}, bf16[128,128,128]{2,1,0:T(8,128)(2,1)}, f32[128,128]{1,0:T(8,128)}, f...) custom-call(s32[2]{0:T(128)} %pad_add_fusion.1.idx_ref, bf16[128,128,512]{2,1,0:T(8,128)(2,1)} %get-tuple-element.54.a_ref.refs_4_, ...), custom_call_target="tpu_custom_call" | custom-call | flops 24999999488 | bytes 50331648 | tf_op jit(solution)/shard_map/middle/pallas_call | solution.py:216
  504.6 27.0 %shard_map.214.refs_12_.da_ref = bf16[128,128,512]{2,1,0:T(8,128)(2,1)} custom-call(bf16[128,64,128]{2,1,0:T(8,128)(2,1)} %get-tuple-element.74.refs_0_, bf16[128,64,128]{2,1,0:T(8,128)(2,1)} %get-tuple-element.75.refs_1_, bf16[128,32,512]{2,1,0:T(8,128)(2,1)} %get-tuple-element.68.refs_0_.refs_2_, bf16[128,32,512]{2,1,0:T(8,128)(2,1)} %get-tuple-element.72.refs_1_.refs_3_, ...), custom_call_target="tpu_custom_call" | custom-call | flops 12000000000 | bytes 83886080 | tf_op jit(solution)/shard_map/pallas_call | solution.py:303
  533.4 16.8 %collective-permute-done.20.refs_1_ = bf16[128,64,128]{2,1,0:T(8,128)(2,1)} collective-permute-done((bf16[128,64,128]{2,1,0:T(8,128)(2,1)S(1)}, bf16[128,64,128]{2,1,0:T(8,128)(2,1)}, u32[]{:S(2)}, u32[]{:S(2)}) %collective-permute-start.20) | collective-permute-done | bytes 2097184 | tf_op jit(solution)/shard_map/ppermute | solution.py:413
  550.2 23.3 %shard_map.215.db_ref = bf16[64,128,512]{2,1,0:T(8,128)(2,1)} custom-call(bf16[128,64,128]{2,1,0:T(8,128)(2,1)} %collective-permute-done.19.refs_0_, bf16[128,64,128]{2,1,0:T(8,128)(2,1)} %collective-permute-done.20.refs_1_, bf16[128,32,512]{2,1,0:T(8,128)(2,1)} %get-tuple-element.60.refs_0_.refs_2_, ...), custom_call_target="tpu_custom_call" | custom-call | flops 12000000000 | bytes 83886080 | tf_op jit(solution)/shard_map/pallas_call | solution.py:303
  575.0 48.2 %final.2 = (bf16[128,512,128]{2,1,0:T(8,128)(2,1)}, f32[512,128]{1,0:T(8,128)}, f32[512,128]{1,0:T(8,128)}, f32[2,128,128]{2,1,0:T(8,128)}) custom-call(s32[4]{0:T(128)} %pad_add_fusion.q_ref, bf16[128,512,128]{2,1,0:T(8,128)(2,1)} %z_ref.5, bf16[128,512,128]{2,1,0:T(8,128)(2,1)} %dy_ref.3, bf16[128,128,512]{2,1,0:T(8,128)(2,1)} %shard_map.214.refs_12_.da_ref, ...), custom_call_target="tpu_custom_call" | custom-call | flops 30000001024 | bytes 67108864 | tf_op jit(solution)/shard_map/final/pallas_call | solution.py:390
  623.3 16.4 %collective-permute-done.14.refs_1_ = bf16[128,64,128]{2,1,0:T(8,128)(2,1)} collective-permute-done((bf16[128,64,128]{2,1,0:T(8,128)(2,1)}, bf16[128,64,128]{2,1,0:T(8,128)(2,1)}, u32[]{:S(2)}, u32[]{:S(2)}) %collective-permute-start.14) | collective-permute-done | bytes 2097184 | tf_op jit(solution)/shard_map/ppermute | solution.py:413
  639.7 23.3 %shard_map.216.db_ref = bf16[64,128,512]{2,1,0:T(8,128)(2,1)} custom-call(bf16[128,64,128]{2,1,0:T(8,128)(2,1)} %collective-permute-done.13.refs_0_, bf16[128,64,128]{2,1,0:T(8,128)(2,1)} %collective-permute-done.14.refs_1_, bf16[128,32,512]{2,1,0:T(8,128)(2,1)} %get-tuple-element.60.refs_0_.refs_2_, ...), custom_call_target="tpu_custom_call" | custom-call | flops 12000000000 | bytes 83886080 | tf_op jit(solution)/shard_map/pallas_call | solution.py:303
  663.0 48.4 %final.3 = (bf16[128,512,128]{2,1,0:T(8,128)(2,1)}, f32[512,128]{1,0:T(8,128)}, f32[512,128]{1,0:T(8,128)}, f32[2,128,128]{2,1,0:T(8,128)}) custom-call(s32[4]{0:T(128)} %pad_add_fusion.q_ref, bf16[128,512,128]{2,1,0:T(8,128)(2,1)} %z_ref.5, bf16[128,512,128]{2,1,0:T(8,128)(2,1)} %dy_ref.3, ...), custom_call_target="tpu_custom_call", output_to_operand_aliasing={{0}: (16, {})} | custom-call | flops 30000001024 | bytes 67108864 | tf_op jit(solution)/shard_map/final/pallas_call | solution.py:390
  713.5 16.5 %all-reduce.2 = (bf16[128]{0:T(256)(128)(2,1)}, bf16[128]{0:T(256)(128)(2,1)}, bf16[512,128]{1,0:T(8,128)(2,1)S(1)}, bf16[512]{0:T(512)(128)(2,1)S(1)}, bf16[128...) all-reduce(f32[128]{0:T(128)S(1)} %get-tuple-element.148, ...), channel_id=1, replica_groups=mesh['batch'=2,'dap'=4] {'dap'}, use_global_device_ids=true, to_apply=%region_1.0 | all-reduce | flops 99584 | bytes 597504 | tf_op jit(solution)/shard_map/psum | solution.py:472
  (119 shorter events, 27.4 us)
Async XLA Ops:
  8.8 44.8 %copy-start.8 = (s32[128,4,1,128]{3,2,1,0:T(1,128)S(1)}, s32[128,4,1,128]{3,2,1,0:T(1,128)}, u32[]{:S(2)}) copy-start(s32[128,4,1,128]{3,2,1,0:T(1,128)} %reshape.48.mask_ref) | copy-start | bytes 786436
  52.8 64.0 %collective-permute-start.3 = (bf16[128,128,512]{2,1,0:T(8,128)(2,1)}, bf16[128,128,512]{2,1,0:T(8,128)(2,1)}, u32[]{:S(2)}, u32[]{:S(2)}) collective-permute-start(bf16[128,128,512]{2,1,0:T(8,128)(2,1)} %get-tuple-element.55.refs_0_.refs_6_), channel_id=1, source_target_pairs={{0,1},{1,0},{2,3},{3,2},{4,5},{5,4},{6,7},{7,6}} | collective-permute-start | bytes 50331656 | tf_op jit(solution)/shard_map/ppermute | solution.py:413
  53.5 204.1 %collective-permute-start.9 = (bf16[128,128,512]{2,1,0:T(8,128)(2,1)}, bf16[128,128,512]{2,1,0:T(8,128)(2,1)}, u32[]{:S(2)}, u32[]{:S(2)}) collective-permute-start(bf16[128,128,512]{2,1,0:T(8,128)(2,1)} %get-tuple-element.54.a_ref.refs_4_), channel_id=1, source_target_pairs={{0,1},{1,0},{2,3},{3,2},{4,5},{5,4},{6,7},{7,6}} | collective-permute-start | bytes 50331656 | tf_op jit(solution)/shard_map/ppermute | solution.py:413
  53.6 103.7 %collective-permute-start.1 = (s32[128,4,1,128]{3,2,1,0:T(1,128)S(1)}, s32[128,4,1,128]{3,2,1,0:T(1,128)S(1)}, u32[]{:S(2)}, u32[]{:S(2)}) collective-permute-start(s32[128,4,1,128]{3,2,1,0:T(1,128)S(1)} %copy-done.8), channel_id=1, source_target_pairs={{0,2},{1,3},{2,0},{3,1},{4,6},{5,7},{6,4},{7,5}} | collective-permute-start | bytes 786440 | tf_op jit(solution)/shard_map/ppermute | solution.py:413
  61.2 96.1 %collective-permute-start.2 = (bf16[32,512,128]{2,1,0:T(8,128)(2,1)}, bf16[32,512,128]{2,1,0:T(8,128)(2,1)}, u32[]{:S(2)}, u32[]{:S(2)}) collective-permute-start(bf16[32,512,128]{2,1,0:T(8,128)(2,1)} %slice.31), channel_id=1, source_target_pairs={{0,2},{1,3},{2,0},{3,1},{4,6},{5,7},{6,4},{7,5}} | collective-permute-start | bytes 12582920 | tf_op jit(solution)/shard_map/ppermute | solution.py:413
  70.3 173.4 %collective-permute-start.4 = (bf16[32,512,128]{2,1,0:T(8,128)(2,1)}, bf16[32,512,128]{2,1,0:T(8,128)(2,1)}, u32[]{:S(2)}, u32[]{:S(2)}) collective-permute-start(bf16[32,512,128]{2,1,0:T(8,128)(2,1)} %get-tuple-element.141), channel_id=1, source_target_pairs={{0,2},{1,3},{2,0},{3,1},{4,6},{5,7},{6,4},{7,5}} | collective-permute-start | bytes 12582920 | tf_op jit(solution)/shard_map/ppermute | solution.py:413
  171.4 126.9 %collective-permute-start.5 = (bf16[128,32,512]{2,1,0:T(8,128)(2,1)}, bf16[128,32,512]{2,1,0:T(8,128)(2,1)}, u32[]{:S(2)}, u32[]{:S(2)}) collective-permute-start(bf16[128,32,512]{2,1,0:T(8,128)(2,1)} %get-tuple-element.59.refs_0_.refs_8_), channel_id=1, source_target_pairs={{0,1},{1,0},{2,3},{3,2},{4,5},{5,4},{6,7},{7,6}} | collective-permute-start | bytes 12582920 | tf_op jit(solution)/shard_map/ppermute | solution.py:413
  257.1 41.1 %collective-permute-start.6 = (bf16[128,32,512]{2,1,0:T(8,128)(2,1)}, bf16[128,32,512]{2,1,0:T(8,128)(2,1)}, u32[]{:S(2)}, u32[]{:S(2)}) collective-permute-start(bf16[128,32,512]{2,1,0:T(8,128)(2,1)} %get-tuple-element.61.refs_1_.refs_9_), channel_id=1, source_target_pairs={{0,1},{1,0},{2,3},{3,2},{4,5},{5,4},{6,7},{7,6}} | collective-permute-start | bytes 12582920 | tf_op jit(solution)/shard_map/ppermute | solution.py:413
  257.1 10.5 %collective-permute-start.7 = (bf16[128,64,128]{2,1,0:T(8,128)(2,1)S(1)}, bf16[128,64,128]{2,1,0:T(8,128)(2,1)}, u32[]{:S(2)}, u32[]{:S(2)}) collective-permute-start(bf16[128,64,128]{2,1,0:T(8,128)(2,1)S(1)} %copy-done.1), channel_id=1, source_target_pairs={{0,1},{1,0},{2,3},{3,2},{4,5},{5,4},{6,7},{7,6}} | collective-permute-start | bytes 6291464 | tf_op jit(solution)/shard_map/ppermute | solution.py:413
  257.7 13.0 %collective-permute-start.8 = (bf16[128,64,128]{2,1,0:T(8,128)(2,1)}, bf16[128,64,128]{2,1,0:T(8,128)(2,1)}, u32[]{:S(2)}, u32[]{:S(2)}) collective-permute-start(bf16[128,64,128]{2,1,0:T(8,128)(2,1)} %get-tuple-element.65.refs_3_), channel_id=1, source_target_pairs={{0,1},{1,0},{2,3},{3,2},{4,5},{5,4},{6,7},{7,6}} | collective-permute-start | bytes 6291464 | tf_op jit(solution)/shard_map/ppermute | solution.py:413
  257.7 93.8 %collective-permute-start = (bf16[32,512,128]{2,1,0:T(8,128)(2,1)}, bf16[32,512,128]{2,1,0:T(8,128)(2,1)}, u32[]{:S(2)}, u32[]{:S(2)}) collective-permute-start(bf16[32,512,128]{2,1,0:T(8,128)(2,1)} %get-tuple-element.142), channel_id=1, source_target_pairs={{0,2},{1,3},{2,0},{3,1},{4,6},{5,7},{6,4},{7,5}} | collective-permute-start | bytes 12582920 | tf_op jit(solution)/shard_map/ppermute | solution.py:413
  267.6 173.2 %collective-permute-start.10 = (bf16[32,512,128]{2,1,0:T(8,128)(2,1)}, bf16[32,512,128]{2,1,0:T(8,128)(2,1)}, u32[]{:S(2)}, u32[]{:S(2)}) collective-permute-start(bf16[32,512,128]{2,1,0:T(8,128)(2,1)} %get-tuple-element.140), channel_id=1, source_target_pairs={{0,2},{1,3},{2,0},{3,1},{4,6},{5,7},{6,4},{7,5}} | collective-permute-start | bytes 12582920 | tf_op jit(solution)/shard_map/ppermute | solution.py:413
  270.6 186.2 %collective-permute-start.15 = (bf16[128,32,512]{2,1,0:T(8,128)(2,1)}, bf16[128,32,512]{2,1,0:T(8,128)(2,1)}, u32[]{:S(2)}, u32[]{:S(2)}) collective-permute-start(bf16[128,32,512]{2,1,0:T(8,128)(2,1)} %get-tuple-element.60.refs_0_.refs_2_), channel_id=1, source_target_pairs={{0,1},{1,0},{2,3},{3,2},{4,5},{5,4},{6,7},{7,6}} | collective-permute-start | bytes 12582920 | tf_op jit(solution)/shard_map/ppermute | solution.py:413
  364.8 93.2 %collective-permute-start.11 = (bf16[128,32,512]{2,1,0:T(8,128)(2,1)}, bf16[128,32,512]{2,1,0:T(8,128)(2,1)}, u32[]{:S(2)}, u32[]{:S(2)}) collective-permute-start(bf16[128,32,512]{2,1,0:T(8,128)(2,1)} %get-tuple-element.68.refs_0_.refs_2_), channel_id=1, source_target_pairs={{0,1},{1,0},{2,3},{3,2},{4,5},{5,4},{6,7},{7,6}} | collective-permute-start | bytes 12582920 | tf_op jit(solution)/shard_map/ppermute | solution.py:413
  398.5 55.7 %copy-start.5 = (s32[128,512]{1,0:T(8,128)S(1)}, s32[128,512]{1,0:T(8,128)}, u32[]{:S(2)}) copy-start(s32[128,512]{1,0:T(8,128)} %param.14) | copy-start | bytes 786436
  398.5 56.4 %copy-start.3 = (bf16[128,8,4,16]{0,3,2,1:T(8,128)(2,1)S(1)}, bf16[128,8,4,16]{0,3,2,1:T(8,128)(2,1)}, u32[]{:S(2)}) copy-start(bf16[128,8,4,16]{0,3,2,1:T(8,128)(2,1)} %copy-done.2) | copy-start | bytes 393220
  398.5 57.1 %copy-start.12 = (bf16[128,128]{1,0:T(8,128)(2,1)S(1)}, bf16[128,128]{1,0:T(8,128)(2,1)}, u32[]{:S(2)}) copy-start(bf16[128,128]{1,0:T(8,128)(2,1)} %param.24) | copy-start | bytes 98308
  398.5 63.2 %copy-start = (bf16[128,64,128]{2,1,0:T(8,128)(2,1)S(1)}, bf16[128,64,128]{2,1,0:T(8,128)(2,1)}, u32[]{:S(2)}) copy-start(bf16[128,64,128]{2,1,0:T(8,128)(2,1)} %get-tuple-element.70.refs_5_) | copy-start | bytes 6291460
  454.2 7.5 %collective-permute-start.12 = (bf16[128,32,512]{2,1,0:T(8,128)(2,1)}, bf16[128,32,512]{2,1,0:T(8,128)(2,1)}, u32[]{:S(2)}, u32[]{:S(2)}) collective-permute-start(bf16[128,32,512]{2,1,0:T(8,128)(2,1)} %get-tuple-element.72.refs_1_.refs_3_), channel_id=1, source_target_pairs={{0,1},{1,0},{2,3},{3,2},{4,5},{5,4},{6,7},{7,6}} | collective-permute-start | bytes 12582920 | tf_op jit(solution)/shard_map/ppermute | solution.py:413
  456.3 75.3 %collective-permute-start.16 = (bf16[128,32,512]{2,1,0:T(8,128)(2,1)}, bf16[128,32,512]{2,1,0:T(8,128)(2,1)}, u32[]{:S(2)}, u32[]{:S(2)}) collective-permute-start(bf16[128,32,512]{2,1,0:T(8,128)(2,1)} %get-tuple-element.66.refs_6_.refs_3_), channel_id=1, source_target_pairs={{0,1},{1,0},{2,3},{3,2},{4,5},{5,4},{6,7},{7,6}} | collective-permute-start | bytes 12582920 | tf_op jit(solution)/shard_map/ppermute | solution.py:413
  456.8 93.4 %collective-permute-start.17 = (bf16[128,32,512]{2,1,0:T(8,128)(2,1)}, bf16[128,32,512]{2,1,0:T(8,128)(2,1)}, u32[]{:S(2)}, u32[]{:S(2)}) collective-permute-start(bf16[128,32,512]{2,1,0:T(8,128)(2,1)} %get-tuple-element.71.refs_12_.refs_4_), channel_id=1, source_target_pairs={{0,1},{1,0},{2,3},{3,2},{4,5},{5,4},{6,7},{7,6}} | collective-permute-start | bytes 12582920 | tf_op jit(solution)/shard_map/ppermute | solution.py:413
  456.8 93.4 %collective-permute-start.18 = (bf16[128,32,512]{2,1,0:T(8,128)(2,1)}, bf16[128,32,512]{2,1,0:T(8,128)(2,1)}, u32[]{:S(2)}, u32[]{:S(2)}) collective-permute-start(bf16[128,32,512]{2,1,0:T(8,128)(2,1)} %get-tuple-element.73.refs_13_.refs_5_), channel_id=1, source_target_pairs={{0,1},{1,0},{2,3},{3,2},{4,5},{5,4},{6,7},{7,6}} | collective-permute-start | bytes 12582920 | tf_op jit(solution)/shard_map/ppermute | solution.py:413
  457.9 45.8 %copy-start.13 = (f32[128,128]{1,0:T(8,128)S(1)}, f32[128,128]{1,0:T(8,128)}, u32[]{:S(2)}) copy-start(f32[128,128]{1,0:T(8,128)} %get-tuple-element.89) | copy-start | bytes 196612
  457.9 45.8 %copy-start.14 = (f32[128,128]{1,0:T(8,128)S(1)}, f32[128,128]{1,0:T(8,128)}, u32[]{:S(2)}) copy-start(f32[128,128]{1,0:T(8,128)} %get-tuple-element.93) | copy-start | bytes 196612
  457.9 45.8 %copy-start.15 = (f32[128,128]{1,0:T(8,128)S(1)}, f32[128,128]{1,0:T(8,128)}, u32[]{:S(2)}) copy-start(f32[128,128]{1,0:T(8,128)} %get-tuple-element.90) | copy-start | bytes 196612
  457.9 45.8 %copy-start.16 = (f32[128,128]{1,0:T(8,128)S(1)}, f32[128,128]{1,0:T(8,128)}, u32[]{:S(2)}) copy-start(f32[128,128]{1,0:T(8,128)} %get-tuple-element.94) | copy-start | bytes 196612
  457.9 45.8 %copy-start.17 = (f32[128,128]{1,0:T(8,128)S(1)}, f32[128,128]{1,0:T(8,128)}, u32[]{:S(2)}) copy-start(f32[128,128]{1,0:T(8,128)} %get-tuple-element.91) | copy-start | bytes 196612
  458.0 45.8 %copy-start.18 = (f32[128,128]{1,0:T(8,128)S(1)}, f32[128,128]{1,0:T(8,128)}, u32[]{:S(2)}) copy-start(f32[128,128]{1,0:T(8,128)} %get-tuple-element.95) | copy-start | bytes 196612
  458.0 74.7 %collective-permute-start.19 = (bf16[128,64,128]{2,1,0:T(8,128)(2,1)}, bf16[128,64,128]{2,1,0:T(8,128)(2,1)}, u32[]{:S(2)}, u32[]{:S(2)}) collective-permute-start(bf16[128,64,128]{2,1,0:T(8,128)(2,1)} %get-tuple-element.69.refs_4_), channel_id=1, source_target_pairs={{0,2},{1,3},{2,0},{3,1},{4,6},{5,7},{6,4},{7,5}} | collective-permute-start | bytes 6291464 | tf_op jit(solution)/shard_map/ppermute | solution.py:413
  461.7 88.5 %collective-permute-start.20 = (bf16[128,64,128]{2,1,0:T(8,128)(2,1)S(1)}, bf16[128,64,128]{2,1,0:T(8,128)(2,1)}, u32[]{:S(2)}, u32[]{:S(2)}) collective-permute-start(bf16[128,64,128]{2,1,0:T(8,128)(2,1)S(1)} %copy-done), channel_id=1, source_target_pairs={{0,3},{1,2},{2,1},{3,0},{4,7},{5,6},{6,5},{7,4}} | collective-permute-start | bytes 6291464 | tf_op jit(solution)/shard_map/ppermute | solution.py:413
  531.6 91.6 %collective-permute-start.13 = (bf16[128,64,128]{2,1,0:T(8,128)(2,1)}, bf16[128,64,128]{2,1,0:T(8,128)(2,1)}, u32[]{:S(2)}, u32[]{:S(2)}) collective-permute-start(bf16[128,64,128]{2,1,0:T(8,128)(2,1)} %get-tuple-element.74.refs_0_), channel_id=1, source_target_pairs={{0,2},{1,3},{2,0},{3,1},{4,6},{5,7},{6,4},{7,5}} | collective-permute-start | bytes 6291464 | tf_op jit(solution)/shard_map/ppermute | solution.py:413
  532.7 107.0 %collective-permute-start.14 = (bf16[128,64,128]{2,1,0:T(8,128)(2,1)}, bf16[128,64,128]{2,1,0:T(8,128)(2,1)}, u32[]{:S(2)}, u32[]{:S(2)}) collective-permute-start(bf16[128,64,128]{2,1,0:T(8,128)(2,1)} %get-tuple-element.75.refs_1_), channel_id=1, source_target_pairs={{0,3},{1,2},{2,1},{3,0},{4,7},{5,6},{6,5},{7,4}} | collective-permute-start | bytes 6291464 | tf_op jit(solution)/shard_map/ppermute | solution.py:413
  (14 other events, 306.1 us)
